TPU v7x, 32 devices: a whole 2x2x4 slice. The times are simulated.
32 devices in a mesh: dp: 16 (over z, y, core), tensor: 2 (over x).
Axes of the slice: x: 2, y: 2, z: 4, core: 2. Of those that a mesh axis runs over, the one named last changes fastest.
Arguments:
- activations: bfloat16 [4096, 27648], P('dp', 'tensor'), may hold values from -6 to 6
- output_gradient: bfloat16 [4096, 5120], P('dp', 'tensor'), may hold values from -6 to 6
- adapter_a: bfloat16 [2, 13824, 128], P('tensor', 'dp'), may hold values from -0.0390625 to 0.0390625
- adapter_b: bfloat16 [128, 5120], P(None, 'tensor'), may hold values from -0.078125 to 0.078125
- log_ratio: float32 [4096], P('dp'), may hold values from -1.5 to 1.5
- lengths: int32 [1, 16], replicated, may hold values from 1 to 256, as said below
- rewards: int32 [1, 16], replicated, may hold values from 0 to 10
Outputs:
- grad_a: float32 [2, 13824, 128], P('tensor', 'dp')
- adapter_b_gradient: float32 [128, 5120], P(None, 'tensor')
- loss: float32 [], replicated
Inputs may be any that keep to these rules, and one draw needn't show every extreme that they name: `lengths`: in every group some rollout has length 256.
All inputs are finite; a program needn't handle non-finite values.
Results may differ from a plain program's by a relative error of at most 0.0067.
Values may be sent and summed in bfloat16 or wider, within the bound.
A program may use at most 64 MiB of HBM per device.

v0:
```python
import functools

import jax
import jax.numpy as jnp
from jax import lax
from jax.experimental import pallas as pl
from jax.experimental.pallas import tpu as pltpu
from jax.sharding import PartitionSpec as P

clip_eps = 0.2
adapter_scale_factor = 2.0


def token_terms(length_row, reward_row, log_ratio, offset):
    reward = reward_row.astype(jnp.float32)
    center = jnp.mean(reward)
    spread = jnp.mean((reward - center) * (reward - center))
    advantage = (reward - center) / jnp.sqrt(spread + 1.0)
    ends = jnp.cumsum(length_row)
    starts = ends - length_row
    slots = jnp.arange(log_ratio.shape[0], dtype=jnp.int32) + offset
    member = ((slots[None, :] >= starts[:, None]) & (slots[None, :] < ends[:, None])).astype(
        jnp.float32
    )
    live = jnp.sum(member, axis=0)
    token_adv = jnp.sum(member * advantage[:, None], axis=0)
    ratio = jnp.exp(log_ratio)
    unclipped = ratio * token_adv
    clipped = jnp.clip(ratio, 1.0 - clip_eps, 1.0 + clip_eps) * token_adv
    token_loss = -jnp.minimum(unclipped, clipped)
    slope = jnp.where(unclipped <= clipped, -unclipped, jnp.zeros_like(unclipped))
    return (live * slope, jnp.sum(live * token_loss), jnp.sum(live))


def plain_local(activations, output_gradient, adapter_a, adapter_b, log_ratio, lengths, rewards):
    tokens = activations.shape[0]
    groups = lengths.shape[0]
    per_group = lax.axis_size("dp") // groups
    position = lax.axis_index("dp")
    group_id = position // per_group
    offset = position % per_group * tokens
    length_row = lax.dynamic_index_in_dim(lengths, group_id, 0, keepdims=False)
    reward_row = lax.dynamic_index_in_dim(rewards, group_id, 0, keepdims=False)
    token_coefficient, loss_local, live_count = token_terms(
        length_row, reward_row, log_ratio, offset
    )
    columns = activations
    partial_low = jnp.dot(
        columns,
        lax.all_gather(adapter_a, "dp", axis=1, tiled=True)[0],
        preferred_element_type=jnp.float32,
    )
    partial_back = lax.dot_general(
        output_gradient, adapter_b, (((1,), (1,)), ((), ())), preferred_element_type=jnp.float32
    )
    low_rank, backward_projection = lax.psum((partial_low, partial_back), "tensor")
    error_rows = (adapter_scale_factor * token_coefficient[:, None] * backward_projection).astype(
        jnp.bfloat16
    )
    weighted_error = token_coefficient[:, None] * low_rank
    local_adapter_b_gradient = adapter_scale_factor * jnp.einsum(
        "tr,td->rd",
        weighted_error,
        output_gradient.astype(jnp.float32),
        precision=lax.Precision.HIGHEST,
    )
    columns = activations
    grad_a = lax.psum_scatter(
        lax.dot_general(
            columns, error_rows, (((0,), (0,)), ((), ())), preferred_element_type=jnp.float32
        ),
        "dp",
        scatter_dimension=0,
        tiled=True,
    )
    grad_b_sum, loss_sum, live_sum = lax.psum(
        (local_adapter_b_gradient, loss_local, live_count), "dp"
    )
    factor = groups / live_sum
    return ((factor * grad_a)[None], factor * grad_b_sum, factor * loss_sum)


MESH = pl.DeviceIdType.MESH
f32, bf16 = jnp.float32, jnp.bfloat16


def tile_of(total, most):
    return max(k for k in range(128, most + 1, 128) if total % k == 0)


def fused_kernel(
    n, groups, rollouts,
    act_hbm, grad_hbm, a_hbm, b_hbm, ratio_ref, len_ref, rew_ref,
    out_a, out_b, out_loss,
    act, grad, b_mat, a_all, part, rs1, rs2, rs3, xs, xr, coef, err,
    gb, gbs, gb1, gb2s, gb2, gb3s, gb3, fin, ls, l1, l2, lz,
    loc, ag_s, ag_r, rs1_s, rs1_r, rs2_s, rs2_r, rs3_s, rs3_r, x_s, x_r,
    g_s, g_r, gz_s, gz_r, fz_s, fz_r, l_s, l_r, lz_s, lz_r,
):
    depth = n // 4
    p = lax.axis_index("dp")
    t = lax.axis_index("tensor")
    c, y, z = p % 2, (p // 2) % 2, p // 4
    tokens, ff = act.shape
    rows, rank = a_hbm.shape

    def at(zz, yy, cc):
        return (zz * 2 + yy) * 2 + cc

    def turn(k):
        return lax.rem(z + (k + depth), depth)

    def block(ref, q):
        return ref.at[pl.ds(pl.multiple_of(q * rows, 16), rows)]

    def remote(s, d, ss, rs, dev, tensor=None):
        return pltpu.make_async_remote_copy(
            src_ref=s, dst_ref=d, send_sem=ss, recv_sem=rs,
            device_id=(dev, t if tensor is None else tensor), device_id_type=MESH,
        )

    core, side = at(z, y, 1 - c), at(z, 1 - y, c)
    zs = [turn(k) for k in range(depth)]
    peer = [at(zs[k], y, c) for k in range(depth)]

    load_a = pltpu.make_async_copy(a_hbm, block(a_all, p), loc.at[0])
    load_g = pltpu.make_async_copy(grad_hbm, grad, loc.at[1])
    load_b = pltpu.make_async_copy(b_hbm, b_mat, loc.at[2])
    load_x = pltpu.make_async_copy(act_hbm, act, loc.at[3])
    for copy in (load_a, load_g, load_b, load_x):
        copy.start()

    barrier = pltpu.get_barrier_semaphore()
    for dev in [core, side] + peer[1:]:
        pl.semaphore_signal(barrier, inc=1, device_id=(dev, t), device_id_type=MESH)
    pl.semaphore_signal(barrier, inc=1, device_id=(p, 1 - t), device_id_type=MESH)
    pl.semaphore_wait(barrier, depth + 2)

    sent = []

    def go(copy):
        copy.start()
        sent.append(copy)
        return copy

    count = [0]

    def gather_send(q, dev):
        go(remote(block(a_all, q), block(a_all, q), ag_s.at[count[0]], ag_r.at[q], dev))
        count[0] += 1

    def gather_wait(q):
        remote(block(a_all, q), block(a_all, q), ag_s.at[0], ag_r.at[q], core).wait_recv()

    load_a.wait()
    far = sorted(range(1, depth), key=lambda k: -min(k, depth - k))
    gather_send(p, side)
    for k in far:
        gather_send(p, peer[k])
    gather_send(p, core)

    load_g.wait()
    load_b.wait()
    xs[0] = lax.dot_general(grad[...], b_mat[...], (((1,), (1,)), ((), ())), preferred_element_type=f32)
    back = go(remote(xs.at[0], xr.at[0], x_s.at[0], x_r.at[0], p, 1 - t))

    per_group = n // groups
    group = p // per_group
    offset = (p % per_group) * tokens
    slots = (
        lax.broadcasted_iota(jnp.int32, ratio_ref.shape, 0) * 128
        + lax.broadcasted_iota(jnp.int32, ratio_ref.shape, 1)
        + offset
    )
    live_total = jnp.int32(0)
    live = jnp.zeros(ratio_ref.shape, f32)
    token_adv = jnp.zeros(ratio_ref.shape, f32)
    for g in range(groups):
        here = jnp.full((1, 128), (group == g).astype(f32))
        reward = [jnp.full((1, 128), rew_ref[g, i]).astype(f32) for i in range(rollouts)]
        center = sum(reward) / rollouts
        spread = sum((r - center) * (r - center) for r in reward) / rollouts
        scale = jnp.sqrt(spread + 1.0)
        end = jnp.int32(0)
        for i in range(rollouts):
            start = end
            end = end + len_ref[g, i]
            member = ((slots >= start) & (slots < end)).astype(f32) * here
            live = live + member
            token_adv = token_adv + member * ((reward[i] - center) / scale)
        live_total = live_total + jnp.minimum(end, per_group * tokens)
    ratio = jnp.exp(ratio_ref[...])
    unclipped = ratio * token_adv
    clipped = jnp.clip(ratio, 1.0 - clip_eps, 1.0 + clip_eps) * token_adv
    token_loss = -jnp.minimum(unclipped, clipped)
    slope = jnp.where(unclipped <= clipped, -unclipped, jnp.zeros_like(unclipped))
    weight = live * slope
    for i in range(tokens // 128):
        coef[pl.ds(i * 128, 128), :] = jnp.broadcast_to(weight[i : i + 1, :], (128, 128)).T
    factor = groups / jnp.full((1, 128), live_total).astype(f32)
    loss_part = jnp.sum(jnp.sum(live * token_loss, axis=1, keepdims=True), axis=0, keepdims=True)

    ls[0] = jnp.broadcast_to(loss_part, (8, 128))
    first = go(remote(ls.at[0], l1, l_s.at[0], l_r.at[0], core))

    back.wait_recv()
    err[...] = (adapter_scale_factor * coef[...] * (xs[0] + xr[0])).astype(bf16)

    load_x.wait()
    tile = tile_of(ff, 1536)
    steps = ff // tile

    def partial_rows(i, _):
        cols = pl.ds(pl.multiple_of(i * tile, 128), tile)
        part[cols, :] = lax.dot_general(
            act[:, cols], err[...], (((0,), (0,)), ((), ())), preferred_element_type=f32
        ).astype(bf16)
        return 0

    near = [depth - k for k in far][::-1]
    for j, k in enumerate(near):
        lax.fori_loop(j * steps // len(near), (j + 1) * steps // len(near), partial_rows, 0)
        q = peer[k]
        gather_wait(q)
        gather_send(q, side)
        gather_send(q, core)

    order = far + [0]
    first_stage = {}
    for yy in (1, 0):
        for k in order:
            yv = 1 - y if yy else y
            i = k * 2 + yy
            first_stage[k, yy] = go(
                remote(block(part, at(zs[k], yv, 1 - c)), rs1.at[i], rs1_s.at[i], rs1_r.at[i], core)
            )

    first.wait_recv()
    ls[1] = ls[0] + l1[...]
    second = go(remote(ls.at[1], l2, l_s.at[1], l_r.at[1], side))

    second_stage = {}
    for k in order:
        first_stage[k, 1].wait_recv()
        own = block(part, at(zs[k], 1 - y, c))
        own[...] = (own[...].astype(f32) + rs1[k * 2 + 1].astype(f32)).astype(bf16)
        second_stage[k] = go(remote(own, rs2.at[k], rs2_s.at[k], rs2_r.at[k], side))

    second.wait_recv()
    lz[z] = ls[1] + l2[...]
    third = [go(remote(lz.at[z], lz.at[z], lz_s.at[k], lz_r.at[k], peer[k])) for k in range(1, depth)]

    for k in [0] + near:
        q = at(zs[k], 1 - y, c)
        gather_wait(q)
        gather_send(q, core)
    for k in range(depth):
        gather_wait(at(zs[k], y, 1 - c))
    for k in range(depth):
        gather_wait(at(zs[k], 1 - y, 1 - c))

    def low_rows(i, total):
        cols = pl.ds(pl.multiple_of(i * tile, 128), tile)
        return total + jnp.dot(act[:, cols], a_all[cols, :], preferred_element_type=f32)

    xs[1] = lax.fori_loop(0, steps, low_rows, jnp.zeros((tokens, rank), f32))
    low = go(remote(xs.at[1], xr.at[1], x_s.at[1], x_r.at[1], p, 1 - t))

    third_stage = {}
    for k in far:
        first_stage[k, 0].wait_recv()
        second_stage[k].wait_recv()
        own = block(part, at(zs[k], y, c))
        own[...] = (
            own[...].astype(f32) + rs1[k * 2].astype(f32) + rs2[k].astype(f32)
        ).astype(bf16)
        third_stage[k] = go(remote(own, rs3.at[k], rs3_s.at[k], rs3_r.at[k], peer[k]))

    low.wait_recv()
    weighted = coef[...] * (xs[1] + xr[1])
    high = weighted.astype(bf16)
    rest = weighted - high.astype(f32)
    middle = rest.astype(bf16)
    last = (rest - middle.astype(f32)).astype(bf16)
    width = grad.shape[1]
    wide = tile_of(width, 640)
    for i in range(width // wide):
        cols = pl.ds(i * wide, wide)
        g = grad[:, cols]
        total = sum(
            lax.dot_general(w, g, (((0,), (0,)), ((), ())), preferred_element_type=f32)
            for w in (last, middle, high)
        )
        gb[:, cols] = total
        gbs[:, cols] = total.astype(bf16)

    half, quarter, chunk = rank // 2, rank // 4, width // depth
    lane = pl.multiple_of(c * half, 16)
    other = pl.multiple_of((1 - c) * half, 16)
    one = go(remote(gbs.at[pl.ds(other, half)], gb1, g_s.at[0], g_r.at[0], core))
    one.wait_recv()
    away = pl.multiple_of((1 - y) * quarter, 16)
    stay = pl.multiple_of(y * quarter, 16)
    mine = pl.multiple_of(lane + stay, 16)
    gb2s[...] = (
        gb[pl.ds(pl.multiple_of(lane + away, 16), quarter), :] + gb1[pl.ds(away, quarter), :].astype(f32)
    ).astype(bf16)
    two = go(remote(gb2s, gb2, g_s.at[1], g_r.at[1], side))

    first_stage[0, 0].wait_recv()
    second_stage[0].wait_recv()
    total = block(part, p)[...].astype(f32) + rs1[0].astype(f32) + rs2[0].astype(f32)
    out_a[...] = total

    two.wait_recv()
    total = (
        gb[pl.ds(mine, quarter), :]
        + gb1[pl.ds(stay, quarter), :].astype(f32)
        + gb2[...].astype(f32)
    )
    gb3s[...] = total.astype(bf16)
    gb[pl.ds(mine, quarter), :] = total

    def chunk_of(zz):
        return pl.ds(pl.multiple_of(zz * chunk, 128), chunk)

    three = {
        k: go(remote(gb3s.at[:, chunk_of(zs[k])], gb3.at[k], gz_s.at[k], gz_r.at[k], peer[k]))
        for k in far
    }

    for k in far:
        third_stage[k].wait_recv()
        out_a[...] = out_a[...] + rs3[k].astype(f32)
    out_a[...] = factor * out_a[...]
    for copy in third:
        copy.wait_recv()
    total = lz[0]
    for i in range(1, depth):
        total = total + lz[i]
    out_loss[...] = factor * total

    for k in far:
        three[k].wait_recv()
    total = gb[pl.ds(mine, quarter), chunk_of(z)]
    for k in far:
        total = total + gb3[k].astype(f32)
    scaled = jnp.full((1, 128), adapter_scale_factor) * factor
    fin[pl.ds(mine, quarter), chunk_of(z)] = (scaled[:, :1] * total).astype(bf16)

    piece = fin.at[pl.ds(mine, quarter), chunk_of(z)]
    four = {k: go(remote(piece, piece, fz_s.at[k], fz_r.at[k], peer[k])) for k in far}
    for k in far:
        four[k].wait_recv()
    piece = fin.at[pl.ds(mine, quarter)]
    five = go(remote(piece, piece, g_s.at[2], g_r.at[2], side))
    five.wait_recv()
    piece = fin.at[pl.ds(lane, half)]
    six = go(remote(piece, piece, g_s.at[3], g_r.at[3], core))
    six.wait_recv()
    out_b[...] = fin[...].astype(f32)
    for copy in sent:
        copy.wait_send()


def fused_local(activations, output_gradient, adapter_a, adapter_b, log_ratio, lengths, rewards):
    n = lax.axis_size("dp")
    depth = n // 4
    tokens, ff = activations.shape
    rows, rank = adapter_a.shape[1:]
    width = output_gradient.shape[1]
    dma = pltpu.SemaphoreType.DMA
    vmem, anywhere = pl.BlockSpec(memory_space=pltpu.VMEM), pl.BlockSpec(memory_space=pl.ANY)
    scalars = pl.BlockSpec(memory_space=pltpu.SMEM)
    quarter, chunk = rank // 4, width // depth
    grad_a, grad_b, loss = pl.pallas_call(
        functools.partial(fused_kernel, n, lengths.shape[0], lengths.shape[1]),
        out_shape=(
            jax.ShapeDtypeStruct((rows, rank), f32),
            jax.ShapeDtypeStruct((rank, width), f32),
            jax.ShapeDtypeStruct((8, 128), f32),
        ),
        in_specs=[anywhere] * 4 + [vmem, scalars, scalars],
        out_specs=(vmem, vmem, vmem),
        scratch_shapes=[
            pltpu.VMEM((tokens, ff), bf16),
            pltpu.VMEM((tokens, width), bf16),
            pltpu.VMEM((rank, width), bf16),
            pltpu.VMEM((ff, rank), bf16),
            pltpu.VMEM((ff, rank), bf16),
            pltpu.VMEM((2 * depth, rows, rank), bf16),
            pltpu.VMEM((depth, rows, rank), bf16),
            pltpu.VMEM((depth, rows, rank), bf16),
            pltpu.VMEM((2, tokens, rank), f32),
            pltpu.VMEM((2, tokens, rank), f32),
            pltpu.VMEM((tokens, rank), f32),
            pltpu.VMEM((tokens, rank), bf16),
            pltpu.VMEM((rank, width), f32),
            pltpu.VMEM((rank, width), bf16),
            pltpu.VMEM((rank // 2, width), bf16),
            pltpu.VMEM((quarter, width), bf16),
            pltpu.VMEM((quarter, width), bf16),
            pltpu.VMEM((quarter, width), bf16),
            pltpu.VMEM((depth, quarter, chunk), bf16),
            pltpu.VMEM((rank, width), bf16),
            pltpu.VMEM((2, 8, 128), f32),
            pltpu.VMEM((8, 128), f32),
            pltpu.VMEM((8, 128), f32),
            pltpu.VMEM((depth, 8, 128), f32),
            dma((4,)), dma((n - 1 + 0,)), dma((n,)),
            dma((2 * depth,)), dma((2 * depth,)),
            dma((depth,)), dma((depth,)), dma((depth,)), dma((depth,)),
            dma((2,)), dma((2,)),
            dma((4,)), dma((4,)), dma((depth,)), dma((depth,)), dma((depth,)), dma((depth,)),
            dma((2,)), dma((2,)), dma((depth,)), dma((depth,)),
        ],
        compiler_params=pltpu.CompilerParams(
            collective_id=0, has_side_effects=True, vmem_limit_bytes=48 * 1024 * 1024
        ),
        name="fused",
    )(
        activations, output_gradient, adapter_a[0], adapter_b,
        log_ratio.reshape(-1, 128), lengths, rewards,
    )
    return grad_a[None], grad_b, loss[0, 0]


def fits(mesh):
    n, split = mesh.shape["dp"], mesh.shape["tensor"]
    return n % 4 == 0 and 4 <= n <= 16 and split == 2


def local(activations, output_gradient, adapter_a, adapter_b, log_ratio, lengths, rewards):
    n = lax.axis_size("dp")
    rows, rank = adapter_a.shape[1:]
    width, ff = output_gradient.shape[1], activations.shape[1]
    small = 2 * activations.size + 8 * ff * rank < 32 * 1024 * 1024
    aligned = (
        rows % 16 == 0
        and rank == 128
        and activations.shape[0] % 128 == 0
        and ff % 128 == 0
        and width % (128 * (n // 4)) == 0
        and n % lengths.shape[0] == 0
    )
    run = fused_local if small and aligned else plain_local
    return run(activations, output_gradient, adapter_a, adapter_b, log_ratio, lengths, rewards)


def solution(mesh):
    in_specs = (
        P("dp", "tensor"),
        P("dp", "tensor"),
        P("tensor", "dp", None),
        P(None, "tensor"),
        P("dp"),
        P(),
        P(),
    )
    out_specs = (P("tensor", "dp", None), P(None, "tensor"), P())
    body = local if fits(mesh) else plain_local
    return jax.shard_map(body, mesh=mesh, in_specs=in_specs, out_specs=out_specs, check_vma=False)
```

profile of v0, /device:TPU:1, one launch (start us, length us, event | category | flops | bytes accessed | tf_op | source)
XLA Modules:
  0.0 88.0 jit_solution(2955415881586334181)
XLA Ops:
  0.6 0.0 copy-start
  0.6 1.3 %copy-done = bf16[256,2560]{1,0:T(8,128)(2,1)S(1)} copy-done((bf16[256,2560]{1,0:T(8,128)(2,1)S(1)}, bf16[256,2560]{1,0:T(8,128)(2,1)}, u32[]{:S(2)}) %copy-start) | copy-done | bytes 1310744
  1.9 0.0 copy-start.1
  2.0 1.1 %copy-done.1 = bf16[128,2560]{1,0:T(8,128)(2,1)S(1)} copy-done((bf16[128,2560]{1,0:T(8,128)(2,1)S(1)}, bf16[128,2560]{1,0:T(8,128)(2,1)}, u32[]{:S(2)}) %copy-start.1) | copy-done | bytes 655384
  3.0 0.0 copy-start.2
  3.0 0.9 %copy-done.2 = bf16[1,864,128]{2,1,0:T(8,128)(2,1)S(1)} copy-done((bf16[1,864,128]{2,1,0:T(8,128)(2,1)S(1)}, bf16[1,864,128]{2,1,0:T(8,128)(2,1)}, u32[]{:S(2)}) %copy-start.2) | copy-done | bytes 221208
  4.0 0.0 copy-start.3
  4.0 0.7 copy-done.3
  4.7 0.0 copy-start.4
  4.7 0.7 copy-done.4
  5.3 0.0 copy-start.5
  5.3 0.7 copy-done.5
  6.0 79.7 %fused.1 = (f32[864,128]{1,0:T(8,128)S(1)}, f32[128,2560]{1,0:T(8,128)S(1)}, f32[8,128]{1,0:T(8,128)S(1)}) custom-call(bf16[256,13824]{1,0:T(8,128)(2,1)} %act_hbm.1, bf16[256,2560]{1,0:T(8,128)(2,1)S(1)} %copy-done, bf16[864,128]{1,0:T(8,128)(2,1)S(1)} %bitcast.5, bf16[128,2560]{1,0:T(8,128)(2,1)S(1)} %copy-done.1, f32[2,128]{1,0:T(2,128)S(1)} %bitcast.6, ...), custom_call_target="tpu_custom_call" | custom-call | tf_op jit(solution)/shard_map/fused/pallas_call | solution.py:376
  85.7 0.5 slice.3
  86.2 0.8 copy.12
  86.9 1.1 %copy.13 = f32[128,2560]{1,0:T(8,128)} copy(f32[128,2560]{1,0:T(8,128)S(1)} %get-tuple-element.13) | data formatting | bytes 2621440
Async XLA Ops:
  0.6 1.3 %copy-start = (bf16[256,2560]{1,0:T(8,128)(2,1)S(1)}, bf16[256,2560]{1,0:T(8,128)(2,1)}, u32[]{:S(2)}) copy-start(bf16[256,2560]{1,0:T(8,128)(2,1)} %grad_hbm.1) | copy-start | bytes 3932164
  1.9 1.1 %copy-start.1 = (bf16[128,2560]{1,0:T(8,128)(2,1)S(1)}, bf16[128,2560]{1,0:T(8,128)(2,1)}, u32[]{:S(2)}) copy-start(bf16[128,2560]{1,0:T(8,128)(2,1)} %b_hbm.1) | copy-start | bytes 1966084
  3.0 0.9 %copy-start.2 = (bf16[1,864,128]{2,1,0:T(8,128)(2,1)S(1)}, bf16[1,864,128]{2,1,0:T(8,128)(2,1)}, u32[]{:S(2)}) copy-start(bf16[1,864,128]{2,1,0:T(8,128)(2,1)} %param.9) | copy-start | bytes 663556
  4.0 0.7 copy-start.3
  4.7 0.7 copy-start.4
  5.3 0.7 copy-start.5
where the time goes:
time: 88.3 us; the launch traced here: 88 us
  Pallas kernels  79.7 us (90%)
  local copies, waits for them, and re-layouts  7.65 us (9%)
    pallas_call x1, Pallas kernels, fused_local(): pl.pallas_call(functools.partial(fused_kernel, n, lengths.shape[0], lengt...  79.7 us
    unnamed x14, local copies, waits for them, and re-layouts  7.14 us

commit v1 on v0

--- a/solution.py
+++ b/solution.py
@@ -90,8 +90,9 @@
 
 def fused_kernel(
     n, groups, rollouts,
-    act_hbm, grad_hbm, a_hbm, b_hbm, ratio_ref, len_ref, rew_ref,
+    act_hbm, grad_hbm, a_hbm, b_hbm, ratio_hbm, len_hbm, rew_hbm,
     out_a, out_b, out_loss,
+    ratio_ref, len_ref, rew_ref,
     act, grad, b_mat, a_all, part, rs1, rs2, rs3, xs, xr, coef, err,
     gb, gbs, gb1, gb2s, gb2, gb3s, gb3, fin, ls, l1, l2, lz,
     loc, ag_s, ag_r, rs1_s, rs1_r, rs2_s, rs2_r, rs3_s, rs3_r, x_s, x_r,
@@ -127,13 +128,20 @@
     load_g = pltpu.make_async_copy(grad_hbm, grad, loc.at[1])
     load_b = pltpu.make_async_copy(b_hbm, b_mat, loc.at[2])
     load_x = pltpu.make_async_copy(act_hbm, act, loc.at[3])
-    for copy in (load_a, load_g, load_b, load_x):
-        copy.start()
-
+    small = [
+        pltpu.make_async_copy(s, d, loc.at[4 + i])
+        for i, (s, d) in enumerate(((ratio_hbm, ratio_ref), (len_hbm, len_ref), (rew_hbm, rew_ref)))
+    ]
     barrier = pltpu.get_barrier_semaphore()
     for dev in [core, side] + peer[1:]:
         pl.semaphore_signal(barrier, inc=1, device_id=(dev, t), device_id_type=MESH)
     pl.semaphore_signal(barrier, inc=1, device_id=(p, 1 - t), device_id_type=MESH)
+    for copy in [load_a, load_g, load_b] + small + [load_x]:
+        copy.start()
+    load_g.wait()
+    load_b.wait()
+    xs[0] = lax.dot_general(grad[...], b_mat[...], (((1,), (1,)), ((), ())), preferred_element_type=f32)
+    load_a.wait()
     pl.semaphore_wait(barrier, depth + 2)
 
     sent = []
@@ -152,18 +160,16 @@
     def gather_wait(q):
         remote(block(a_all, q), block(a_all, q), ag_s.at[0], ag_r.at[q], core).wait_recv()
 
-    load_a.wait()
     far = sorted(range(1, depth), key=lambda k: -min(k, depth - k))
     gather_send(p, side)
     for k in far:
         gather_send(p, peer[k])
     gather_send(p, core)
 
-    load_g.wait()
-    load_b.wait()
-    xs[0] = lax.dot_general(grad[...], b_mat[...], (((1,), (1,)), ((), ())), preferred_element_type=f32)
     back = go(remote(xs.at[0], xr.at[0], x_s.at[0], x_r.at[0], p, 1 - t))
 
+    for copy in small:
+        copy.wait()
     per_group = n // groups
     group = p // per_group
     offset = (p % per_group) * tokens
@@ -363,6 +369,18 @@
         copy.wait_send()
 
 
+def finish_kernel(a_in, b_in, loss_in, a_out, b_out, loss_out, sems):
+    copies = [
+        pltpu.make_async_copy(s, d, sems.at[i])
+        for i, (s, d) in enumerate(((a_in, a_out), (b_in, b_out)))
+    ]
+    for copy in copies:
+        copy.start()
+    loss_out[0, 0] = loss_in[0, 0]
+    for copy in copies:
+        copy.wait()
+
+
 def fused_local(activations, output_gradient, adapter_a, adapter_b, log_ratio, lengths, rewards):
     n = lax.axis_size("dp")
     depth = n // 4
@@ -372,6 +390,7 @@
     dma = pltpu.SemaphoreType.DMA
     vmem, anywhere = pl.BlockSpec(memory_space=pltpu.VMEM), pl.BlockSpec(memory_space=pl.ANY)
     scalars = pl.BlockSpec(memory_space=pltpu.SMEM)
+    hbm = pl.BlockSpec(memory_space=pltpu.HBM)
     quarter, chunk = rank // 4, width // depth
     grad_a, grad_b, loss = pl.pallas_call(
         functools.partial(fused_kernel, n, lengths.shape[0], lengths.shape[1]),
@@ -380,9 +399,12 @@
             jax.ShapeDtypeStruct((rank, width), f32),
             jax.ShapeDtypeStruct((8, 128), f32),
         ),
-        in_specs=[anywhere] * 4 + [vmem, scalars, scalars],
+        in_specs=[hbm] * 7,
         out_specs=(vmem, vmem, vmem),
         scratch_shapes=[
+            pltpu.VMEM((tokens // 128, 128), f32),
+            pltpu.SMEM(lengths.shape, jnp.int32),
+            pltpu.SMEM(rewards.shape, jnp.int32),
             pltpu.VMEM((tokens, ff), bf16),
             pltpu.VMEM((tokens, width), bf16),
             pltpu.VMEM((rank, width), bf16),
@@ -407,7 +429,7 @@
             pltpu.VMEM((8, 128), f32),
             pltpu.VMEM((8, 128), f32),
             pltpu.VMEM((depth, 8, 128), f32),
-            dma((4,)), dma((n - 1 + 0,)), dma((n,)),
+            dma((7,)), dma((n - 1 + 0,)), dma((n,)),
             dma((2 * depth,)), dma((2 * depth,)),
             dma((depth,)), dma((depth,)), dma((depth,)), dma((depth,)),
             dma((2,)), dma((2,)),
@@ -419,10 +441,28 @@
         ),
         name="fused",
     )(
-        activations, output_gradient, adapter_a[0], adapter_b,
-        log_ratio.reshape(-1, 128), lengths, rewards,
-    )
-    return grad_a[None], grad_b, loss[0, 0]
+        *(
+            pltpu.with_memory_space_constraint(v, pltpu.HBM)
+            for v in (
+                activations, output_gradient, adapter_a[0], adapter_b,
+                log_ratio.reshape(-1, 128), lengths, rewards,
+            )
+        )
+    )
+    grad_a, grad_b, loss = pl.pallas_call(
+        finish_kernel,
+        out_shape=(
+            jax.ShapeDtypeStruct((rows, rank), f32),
+            jax.ShapeDtypeStruct((rank, width), f32),
+            jax.ShapeDtypeStruct((1, 1), f32),
+        ),
+        in_specs=[vmem, vmem, vmem],
+        out_specs=(hbm, hbm, scalars),
+        scratch_shapes=[dma((2,))],
+        compiler_params=pltpu.CompilerParams(vmem_limit_bytes=4 * 1024 * 1024),
+        name="finish",
+    )(grad_a, grad_b, loss)
+    return grad_a[None], grad_b, loss.reshape(())
 
 
 def fits(mesh):

time: 88.3 us -> 82 us (0.929)
  local copies, waits for them, and re-layouts: 7.65 us -> 0 us
  Pallas kernels: 79.7 us -> 81.2 us
    unnamed x14 -> x0, local copies, waits for them, and re-layouts: 7.14 us -> none
    pallas_call x0 -> x1, Pallas kernels: none -> 1.74 us  [fused_local(): pl.pallas_call(finish_kernel, out_shape=(jax.ShapeDtypeStruct((rows, rank...]
where the time goes in v1:
time: 82 us; the launch traced here: 81.9 us
  Pallas kernels  81.2 us (99%)
    pallas_call x1, Pallas kernels, fused_local(): pl.pallas_call(functools.partial(fused_kernel, n, lengths.shape[0], lengt...  79.5 us
    pallas_call x1, Pallas kernels, fused_local(): pl.pallas_call(finish_kernel, out_shape=(jax.ShapeDtypeStruct((rows, rank...  1.74 us

profile of v1, /device:TPU:1, one launch (start us, length us, event | category | flops | bytes accessed | tf_op | source)
XLA Modules:
  0.0 81.9 jit_solution(2519469071964974895)
XLA Ops:
  0.6 79.5 %fused.1 = (f32[864,128]{1,0:T(8,128)S(1)}, f32[128,2560]{1,0:T(8,128)S(1)}, f32[8,128]{1,0:T(8,128)S(1)}) custom-call(bf16[256,13824]{1,0:T(8,128)(2,1)} %act_hbm.1, bf16[256,2560]{1,0:T(8,128)(2,1)} %grad_hbm.1, bf16[864,128]{1,0:T(8,128)(2,1)} %bitcast.4, bf16[128,2560]{1,0:T(8,128)(2,1)} %b_hbm.1, f32[2,128]{1,0:T(2,128)} %bitcast.5, s32[1,16]{1,0:T(1,128)} %len_hbm.1, ...), custom_call_target="tpu_custom_call" | custom-call | tf_op jit(solution)/shard_map/fused/pallas_call | solution.py:395
  80.1 1.7 %finish.1 = (f32[864,128]{1,0:T(8,128)}, f32[128,2560]{1,0:T(8,128)}, f32[1,1]{1,0:T(1,128)}) custom-call(f32[864,128]{1,0:T(8,128)S(1)} %get-tuple-element.9.a_in, f32[128,2560]{1,0:T(8,128)S(1)} %get-tuple-element.10.b_in, f32[8,128]{1,0:T(8,128)S(1)} %get-tuple-element.11.loss_in), custom_call_target="tpu_custom_call" | custom-call | tf_op jit(solution)/shard_map/finish/pallas_call | solution.py:452

commit v2 on v1

v2 whole, which is shorter than its diff:
```python
import contextlib
import functools

import jax
import jax.numpy as jnp
from jax import lax
from jax.experimental import pallas as pl
from jax.experimental.pallas import tpu as pltpu
from jax.sharding import PartitionSpec as P

clip_eps = 0.2
adapter_scale_factor = 2.0


def token_terms(length_row, reward_row, log_ratio, offset):
    reward = reward_row.astype(jnp.float32)
    center = jnp.mean(reward)
    spread = jnp.mean((reward - center) * (reward - center))
    advantage = (reward - center) / jnp.sqrt(spread + 1.0)
    ends = jnp.cumsum(length_row)
    starts = ends - length_row
    slots = jnp.arange(log_ratio.shape[0], dtype=jnp.int32) + offset
    member = ((slots[None, :] >= starts[:, None]) & (slots[None, :] < ends[:, None])).astype(
        jnp.float32
    )
    live = jnp.sum(member, axis=0)
    token_adv = jnp.sum(member * advantage[:, None], axis=0)
    ratio = jnp.exp(log_ratio)
    unclipped = ratio * token_adv
    clipped = jnp.clip(ratio, 1.0 - clip_eps, 1.0 + clip_eps) * token_adv
    token_loss = -jnp.minimum(unclipped, clipped)
    slope = jnp.where(unclipped <= clipped, -unclipped, jnp.zeros_like(unclipped))
    return (live * slope, jnp.sum(live * token_loss), jnp.sum(live))


def plain_local(activations, output_gradient, adapter_a, adapter_b, log_ratio, lengths, rewards):
    tokens = activations.shape[0]
    groups = lengths.shape[0]
    per_group = lax.axis_size("dp") // groups
    position = lax.axis_index("dp")
    group_id = position // per_group
    offset = position % per_group * tokens
    length_row = lax.dynamic_index_in_dim(lengths, group_id, 0, keepdims=False)
    reward_row = lax.dynamic_index_in_dim(rewards, group_id, 0, keepdims=False)
    token_coefficient, loss_local, live_count = token_terms(
        length_row, reward_row, log_ratio, offset
    )
    columns = activations
    partial_low = jnp.dot(
        columns,
        lax.all_gather(adapter_a, "dp", axis=1, tiled=True)[0],
        preferred_element_type=jnp.float32,
    )
    partial_back = lax.dot_general(
        output_gradient, adapter_b, (((1,), (1,)), ((), ())), preferred_element_type=jnp.float32
    )
    low_rank, backward_projection = lax.psum((partial_low, partial_back), "tensor")
    error_rows = (adapter_scale_factor * token_coefficient[:, None] * backward_projection).astype(
        jnp.bfloat16
    )
    weighted_error = token_coefficient[:, None] * low_rank
    local_adapter_b_gradient = adapter_scale_factor * jnp.einsum(
        "tr,td->rd",
        weighted_error,
        output_gradient.astype(jnp.float32),
        precision=lax.Precision.HIGHEST,
    )
    columns = activations
    grad_a = lax.psum_scatter(
        lax.dot_general(
            columns, error_rows, (((0,), (0,)), ((), ())), preferred_element_type=jnp.float32
        ),
        "dp",
        scatter_dimension=0,
        tiled=True,
    )
    grad_b_sum, loss_sum, live_sum = lax.psum(
        (local_adapter_b_gradient, loss_local, live_count), "dp"
    )
    factor = groups / live_sum
    return ((factor * grad_a)[None], factor * grad_b_sum, factor * loss_sum)


MESH = pl.DeviceIdType.MESH
f32, bf16 = jnp.float32, jnp.bfloat16


def tile_of(total, most):
    return max(k for k in range(128, most + 1, 128) if total % k == 0)


SCOPES = False


def fused_kernel(
    n, groups, rollouts, cut_g, cut_r,
    act_hbm, grad_hbm, a_hbm, b_hbm, ratio_hbm, len_hbm, rew_hbm,
    out_a, out_b, out_loss,
    ratio_ref, len_ref, rew_ref,
    act, grad, b_mat, a_all, part, rs1, rs2, rs3, rs3x, rs4, xs, xr, coef, err,
    gb, gbs, gb1, gb2s, gb2, gb3s, gb3, fin, ls, l1, l2, lz,
    loc, send_s, ag_r, rs1_r, rs2_r, rs3_r, rs3x_r, rs4_r,
    x_r, g1_r, g2_r, g3_r, fin_r, l_r, lz_r,
):
    depth = n // 4
    last = depth - 1
    p = lax.axis_index("dp")
    t = lax.axis_index("tensor")
    c, y, z = p % 2, (p // 2) % 2, p // 4
    tokens, ff = act.shape
    rows, rank = a_hbm.shape
    width = grad.shape[1]
    half, quarter, chunk = rank // 2, rank // 4, width // depth

    def at(zz, yy, cc):
        return (zz * 2 + yy) * 2 + cc

    def remote(s, d, ss, rs, dev, tensor=None):
        return pltpu.make_async_remote_copy(
            src_ref=s, dst_ref=d, send_sem=ss, recv_sem=rs,
            device_id=(dev, t if tensor is None else tensor), device_id_type=MESH,
        )

    core, side = at(z, y, 1 - c), at(z, 1 - y, c)

    load_a = pltpu.make_async_copy(a_hbm, a_all.at[pl.ds(pl.multiple_of(p * rows, 16), rows)], loc.at[0])
    load_g = pltpu.make_async_copy(grad_hbm, grad, loc.at[1])
    load_b = pltpu.make_async_copy(b_hbm, b_mat, loc.at[2])
    load_x = pltpu.make_async_copy(act_hbm, act, loc.at[3])
    small = [
        pltpu.make_async_copy(s, d, loc.at[4 + i])
        for i, (s, d) in enumerate(((ratio_hbm, ratio_ref), (len_hbm, len_ref), (rew_hbm, rew_ref)))
    ]
    barrier = pltpu.get_barrier_semaphore()
    for dev in [core, side] + [at((z + k) % depth, y, c) for k in range(1, depth)]:
        pl.semaphore_signal(barrier, inc=1, device_id=(dev, t), device_id_type=MESH)
    pl.semaphore_signal(barrier, inc=1, device_id=(p, 1 - t), device_id_type=MESH)
    for copy in [load_a, load_g, load_b] + small + [load_x]:
        copy.start()
    load_g.wait()
    load_b.wait()
    xs[0] = lax.dot_general(grad[...], b_mat[...], (((1,), (1,)), ((), ())), preferred_element_type=f32)
    for copy in small:
        copy.wait()

    per_group = n // groups
    group = p // per_group
    offset = (p % per_group) * tokens
    slots = (
        lax.broadcasted_iota(jnp.int32, ratio_ref.shape, 0) * 128
        + lax.broadcasted_iota(jnp.int32, ratio_ref.shape, 1)
        + offset
    )
    live_total = jnp.int32(0)
    live = jnp.zeros(ratio_ref.shape, f32)
    token_adv = jnp.zeros(ratio_ref.shape, f32)
    for g in range(groups):
        here = jnp.full((1, 128), (group == g).astype(f32))
        reward = [jnp.full((1, 128), rew_ref[g, i]).astype(f32) for i in range(rollouts)]
        center = sum(reward) / rollouts
        spread = sum((r - center) * (r - center) for r in reward) / rollouts
        scale = jnp.sqrt(spread + 1.0)
        end = jnp.int32(0)
        for i in range(rollouts):
            start = end
            end = end + len_ref[g, i]
            member = ((slots >= start) & (slots < end)).astype(f32) * here
            live = live + member
            token_adv = token_adv + member * ((reward[i] - center) / scale)
        live_total = live_total + jnp.minimum(end, per_group * tokens)
    ratio = jnp.exp(ratio_ref[...])
    unclipped = ratio * token_adv
    clipped = jnp.clip(ratio, 1.0 - clip_eps, 1.0 + clip_eps) * token_adv
    token_loss = -jnp.minimum(unclipped, clipped)
    slope = jnp.where(unclipped <= clipped, -unclipped, jnp.zeros_like(unclipped))
    weight = live * slope
    for i in range(tokens // 128):
        coef[pl.ds(i * 128, 128), :] = jnp.broadcast_to(weight[i : i + 1, :], (128, 128)).T
    factor = groups / jnp.full((1, 128), live_total).astype(f32)
    loss_part = jnp.sum(jnp.sum(live * token_loss, axis=1, keepdims=True), axis=0, keepdims=True)
    ls[0] = jnp.broadcast_to(loss_part, (8, 128))
    load_a.wait()
    load_x.wait()
    with jax.named_scope("barrier") if SCOPES else contextlib.nullcontext():
        pl.semaphore_wait(barrier, depth + 2)

    flip = (2 * z > last).astype(jnp.int32)
    tile = tile_of(4 * rows, 1280)
    steps = 4 * rows // tile

    def run(u):
        sent = []

        def m(k):
            return k + flip * (last - 2 * k)

        def dev(k, yy, cc):
            return at(m(k), yy, cc)

        others = sorted((k for k in range(depth) if k != u), key=lambda k: abs(k - u))
        up = u + 1 if u < last else None
        down = u - 1 if u > 0 else None

        def onward(k):
            return up if k < u else down

        def go(s, d, rs, device, tensor=None):
            copy = remote(s, d, send_s.at[len(sent)], rs, device, tensor)
            copy.start()
            sent.append(copy)

        def got(d, rs):
            remote(d, d, send_s.at[0], rs, core).wait_recv()

        def z_dev(k):
            return dev(k, y, c)

        def piece(k, yy, cc, i):
            q = dev(k, yy, cc)
            low, size = (0, cut_g) if i == 0 else (cut_g, rows - cut_g)
            return a_all.at[pl.ds(pl.multiple_of(q * rows + low, 16), size)], ag_r.at[2 * q + i]

        def a_send(k, yy, i, *devices):
            ref, sem = piece(k, yy, c, i)
            for device in devices:
                if device is not None:
                    go(ref, ref, sem, device)

        def a_wait(k, yy, cc, i):
            got(*piece(k, yy, cc, i))

        up_dev = None if up is None else z_dev(up)
        down_dev = None if down is None else z_dev(down)

        def a_start():
            a_send(u, y, 0, up_dev, down_dev)
            a_send(u, y, 1, side, up_dev, down_dev)
            a_send(u, y, 0, side)
            a_send(u, y, 0, core)
            a_send(u, y, 1, core)

        def a_side(i):
            a_wait(u, 1 - y, c, i)
            if i == 1:
                a_send(u, 1 - y, 1, up_dev, down_dev)
            a_send(u, 1 - y, i, core)

        def a_line(k, yy, i):
            a_wait(k, yy, c, i)
            to = onward(k)
            a_send(k, yy, i, None if to is None else z_dev(to))
            if i == 0:
                a_send(k, yy, i, side)
            a_send(k, yy, i, core)

        def a_over(k):
            a_wait(k, 1 - y, c, 0)
            a_send(k, 1 - y, 0, core)

        def low_of(k, first):
            for yy in (0, 1):
                for i in (0, 1):
                    a_wait(k, yy, 1 - c, i)
            base = m(k) * (4 * rows)

            def step(i, total):
                cols = pl.ds(pl.multiple_of(base + i * tile, 128), tile)
                return total + jnp.dot(act[:, cols], a_all[cols, :], preferred_element_type=f32)

            begin = jnp.zeros((tokens, rank), f32) if first else xs[1]
            xs[1] = lax.fori_loop(0, steps, step, begin)

        def low_send():
            go(xs.at[1], xr.at[1], x_r.at[1], p, 1 - t)

        def loss_one():
            go(ls.at[0], l1, l_r.at[0], core)

        def loss_two():
            got(l1, l_r.at[0])
            ls[1] = ls[0] + l1[...]
            go(ls.at[1], l2, l_r.at[1], side)

        def loss_three():
            got(l2, l_r.at[1])
            lz[z] = ls[1] + l2[...]
            for k in others:
                go(lz.at[z], lz.at[z], lz_r.at[z], z_dev(k))

        def loss_end():
            for k in others:
                got(lz.at[m(k)], lz_r.at[m(k)])
            total = lz[0]
            for i in range(1, depth):
                total = total + lz[i]
            out_loss[...] = factor * total

        def back_send():
            go(xs.at[0], xr.at[0], x_r.at[0], p, 1 - t)

        def back_end():
            got(xr.at[0], x_r.at[0])
            err[...] = (adapter_scale_factor * coef[...] * (xs[0] + xr[0])).astype(bf16)

        def span(k, yy, cc, part_two=None):
            q = dev(k, yy, cc)
            low, size = {None: (0, rows), 0: (0, cut_r), 1: (cut_r, rows - cut_r)}[part_two]
            return part.at[pl.ds(pl.multiple_of(q * rows + low, 16), size)]

        def part_of(k):
            base = m(k) * (4 * rows)

            def step(i, _):
                cols = pl.ds(pl.multiple_of(base + i * tile, 128), tile)
                part[cols, :] = lax.dot_general(
                    act[:, cols], err[...], (((0,), (0,)), ((), ())), preferred_element_type=f32
                ).astype(bf16)
                return 0

            lax.fori_loop(0, steps, step, 0)
            for yy in (1 - y, y):
                slot = m(k) * 2 + yy
                go(span(k, yy, 1 - c), rs1.at[slot], rs1_r.at[slot], core)

        def both(k, yy, i):
            low, size = (0, cut_r) if i == 0 else (cut_r, rows - cut_r)
            return span(k, yy, c, i)[...].astype(f32) + rs1[m(k) * 2 + yy, pl.ds(low, size), :].astype(f32)

        def core_sum(k):
            for yy in (1 - y, y):
                slot = m(k) * 2 + yy
                got(rs1.at[slot], rs1_r.at[slot])
            ref = span(k, 1 - y, c, 0)
            ref[...] = both(k, 1 - y, 0).astype(bf16)
            go(ref, rs2.at[m(k)], rs2_r.at[m(k)], side)

        def line_slot(k, upward):
            return (flip if upward else 1 - flip) * depth + m(k)

        def sources(k):
            found = []
            if k >= u and down is not None:
                found.append(line_slot(k, True))
            if k <= u and up is not None:
                found.append(line_slot(k, False))
            return found

        def line_x(k):
            total = both(k, 1 - y, 1)
            for slot in sources(k):
                got(rs3x.at[slot], rs3x_r.at[slot])
                total = total + rs3x[slot].astype(f32)
            ref = span(k, 1 - y, c, 1)
            ref[...] = total.astype(bf16)
            if k == u:
                go(ref, rs4, rs4_r.at[0], side)
            else:
                slot = line_slot(k, k > u)
                go(ref, rs3x.at[slot], rs3x_r.at[slot], z_dev(up if k > u else down))

        def line_sum(k):
            slots_in = sources(k)
            got(rs2.at[m(k)], rs2_r.at[m(k)])
            for slot in slots_in:
                got(rs3.at[slot], rs3_r.at[slot])
            first = both(k, y, 0) + rs2[m(k)].astype(f32)
            second = both(k, y, 1)
            for slot in slots_in:
                first = first + rs3[slot, pl.ds(0, cut_r), :].astype(f32)
                second = second + rs3[slot, pl.ds(cut_r, rows - cut_r), :].astype(f32)
            if k == u:
                out_a[pl.ds(0, cut_r), :] = factor * first
                out_a[pl.ds(cut_r, rows - cut_r), :] = second
            else:
                ref = span(k, y, c, 0)
                ref[...] = first.astype(bf16)
                ref = span(k, y, c, 1)
                ref[...] = second.astype(bf16)
                slot = line_slot(k, k > u)
                go(span(k, y, c), rs3.at[slot], rs3_r.at[slot], z_dev(up if k > u else down))

        def a_end():
            got(rs4, rs4_r.at[0])
            rest = pl.ds(cut_r, rows - cut_r)
            out_a[rest, :] = factor * (out_a[rest, :] + rs4[...].astype(f32))

        lane = pl.multiple_of(c * half, 16)
        other = pl.multiple_of((1 - c) * half, 16)
        away = pl.multiple_of((1 - y) * quarter, 16)
        stay = pl.multiple_of(y * quarter, 16)
        mine = pl.multiple_of(lane + stay, 16)
        b_order = others[::-1] + [u]

        def cols_of(k):
            return pl.ds(pl.multiple_of(m(k) * chunk, 128), chunk)

        def b_part():
            got(xr.at[1], x_r.at[1])
            weighted = coef[...] * (xs[1] + xr[1])
            high = weighted.astype(bf16)
            rest = weighted - high.astype(f32)
            middle = rest.astype(bf16)
            last_part = (rest - middle.astype(f32)).astype(bf16)
            for k in b_order:
                cols = cols_of(k)
                total = sum(
                    lax.dot_general(w, grad[:, cols], (((0,), (0,)), ((), ())), preferred_element_type=f32)
                    for w in (last_part, middle, high)
                )
                gb[:, cols] = total
                gbs[:, cols] = total.astype(bf16)
                go(gbs.at[pl.ds(other, half), cols], gb1.at[:, cols], g1_r.at[m(k)], core)

        def b_core(k):
            cols = cols_of(k)
            got(gb1.at[:, cols], g1_r.at[m(k)])
            gb2s[:, cols] = (
                gb[pl.ds(pl.multiple_of(lane + away, 16), quarter), cols]
                + gb1[pl.ds(away, quarter), cols].astype(f32)
            ).astype(bf16)
            go(gb2s.at[:, cols], gb2.at[:, cols], g2_r.at[m(k)], side)

        def b_side(k):
            cols = cols_of(k)
            got(gb2.at[:, cols], g2_r.at[m(k)])
            total = (
                gb[pl.ds(mine, quarter), cols]
                + gb1[pl.ds(stay, quarter), cols].astype(f32)
                + gb2[:, cols].astype(f32)
            )
            if k == u:
                gb[pl.ds(mine, quarter), cols] = total
            else:
                gb3s[:, cols] = total.astype(bf16)
                go(gb3s.at[:, cols], gb3.at[z], g3_r.at[z], z_dev(k))

        def final(k, yy, cc):
            at_row = pl.multiple_of(cc * half + yy * quarter, 16)
            return fin.at[pl.ds(at_row, quarter), cols_of(k)], fin_r.at[dev(k, yy, cc)]

        def b_send(k, yy, *devices):
            ref, sem = final(k, yy, c)
            for device in devices:
                go(ref, ref, sem, device)

        def b_line():
            cols = cols_of(u)
            total = gb[pl.ds(mine, quarter), cols]
            for k in others:
                got(gb3.at[m(k)], g3_r.at[m(k)])
                total = total + gb3[m(k)].astype(f32)
            scaled = jnp.full((1, 128), adapter_scale_factor) * factor
            fin[pl.ds(mine, quarter), cols] = (scaled[:, :1] * total).astype(bf16)
            b_send(u, y, *[z_dev(k) for k in others[::-1]], side, core)

        def b_pass(k, yy):
            got(*final(k, yy, c))
            if yy is y:
                b_send(k, yy, side)
            b_send(k, yy, core)

        def b_end():
            for k in [u] + others:
                for yy in (y, 1 - y):
                    got(*final(k, yy, 1 - c))
            out_b[...] = fin[...].astype(f32)

        there = 1 - y
        plan = [
            (0.0, a_start), (0.1, back_send), (0.2, loss_one),
            (3.0, a_side, 1), (4.5, back_end), (6.4, a_side, 0), (7.2, loss_two), (9.5, loss_three),
        ]
        order = [k for k in (range(last, -1, -1)) if k > u] + [k for k in range(u)] + [u]
        for i, k in enumerate(order):
            plan.append((4.6 + 0.95 * i, part_of, k))
            plan.append((7.05 + 0.95 * i, core_sum, k))
        if u == 0:
            for i, k in enumerate(order[:-1]):
                plan.append(((7.1, 8.1, 12.0)[i % 3], line_x, k))
                plan.append(((11.0, 13.0, 14.0)[i % 3], line_sum, k))
            plan.append((22.0, line_x, u))
            plan.append((30.0, line_sum, u))
        else:
            for k in order:
                if k > u:
                    plan.append((11.5 + 2.0 * (last - k), line_x, k))
                    plan.append((17.0 + 5.0 * (last - k), line_sum, k))
                elif k < u:
                    plan.append((16.0, line_x, k))
                    plan.append((23.5, line_sum, k))
                else:
                    plan.append((20.0, line_x, k))
                    plan.append((30.0, line_sum, k))
        plan.append((31.0, a_end))
        when = {}
        for k in others:
            hops = abs(k - u)
            when[k] = 5.2 + 6.0 * (hops - 1)
            plan.append((when[k], a_line, k, y, 0))
            plan.append((when[k] + 1.2, a_line, k, y, 1))
            plan.append((when[k] + 2.5, a_line, k, there, 1))
            plan.append((when[k] + 5.2, a_over, k))
        for i, k in enumerate([u] + others):
            done = 9.0 if i == 0 else when[k] + 6.4 + 0.1 * i
            plan.append((done, low_of, k, i == 0))
        plan.append((done + 0.1, low_send))
        begin = done + 5.0
        plan.append((begin, b_part))
        for i, k in enumerate(b_order):
            plan.append((begin + 1.5 + 0.01 * i, b_core, k))
            plan.append((begin + 4.5 + 0.9 * i, b_side, k))
        begin = 6.0 * last + 10.6 + 0.1 * last
        plan.append((begin + 9.5, b_line))
        plan.append((begin + 11.5, b_pass, u, there))
        for i, k in enumerate(others):
            plan.append((begin + 12.0 + 0.9 * i, b_pass, k, y))
            plan.append((begin + 14.0 + 0.9 * i, b_pass, k, there))
        plan.append((begin + 18.0, loss_end))
        plan.append((begin + 19.0, b_end))
        for entry in sorted(plan, key=lambda e: e[0]):
            name = entry[1].__name__ + "_".join(str(v) for v in entry[2:] if isinstance(v, int))
            with jax.named_scope(name) if SCOPES else contextlib.nullcontext():
                entry[1](*entry[2:])
        for copy in sent:
            copy.wait_send()

    for u in range((depth + 1) // 2):
        @pl.when(jnp.minimum(z, last - z) == u)
        def _():
            run(u)


def finish_kernel(a_in, b_in, loss_in, a_out, b_out, loss_out, sems):
    copies = [
        pltpu.make_async_copy(s, d, sems.at[i])
        for i, (s, d) in enumerate(((a_in, a_out), (b_in, b_out)))
    ]
    for copy in copies:
        copy.start()
    loss_out[0, 0] = loss_in[0, 0]
    for copy in copies:
        copy.wait()


def fused_local(activations, output_gradient, adapter_a, adapter_b, log_ratio, lengths, rewards):
    n = lax.axis_size("dp")
    depth = n // 4
    tokens, ff = activations.shape
    rows, rank = adapter_a.shape[1:]
    width = output_gradient.shape[1]
    dma = pltpu.SemaphoreType.DMA
    vmem, anywhere = pl.BlockSpec(memory_space=pltpu.VMEM), pl.BlockSpec(memory_space=pl.ANY)
    scalars = pl.BlockSpec(memory_space=pltpu.SMEM)
    hbm = pl.BlockSpec(memory_space=pltpu.HBM)
    quarter, chunk = rank // 4, width // depth
    cut_g, cut_r = rows * 3 // 64 * 16, rows // 32 * 16
    grad_a, grad_b, loss = pl.pallas_call(
        functools.partial(fused_kernel, n, lengths.shape[0], lengths.shape[1], cut_g, cut_r),
        out_shape=(
            jax.ShapeDtypeStruct((rows, rank), f32),
            jax.ShapeDtypeStruct((rank, width), f32),
            jax.ShapeDtypeStruct((8, 128), f32),
        ),
        in_specs=[hbm] * 7,
        out_specs=(vmem, vmem, vmem),
        scratch_shapes=[
            pltpu.VMEM((tokens // 128, 128), f32),
            pltpu.SMEM(lengths.shape, jnp.int32),
            pltpu.SMEM(rewards.shape, jnp.int32),
            pltpu.VMEM((tokens, ff), bf16),
            pltpu.VMEM((tokens, width), bf16),
            pltpu.VMEM((rank, width), bf16),
            pltpu.VMEM((ff, rank), bf16),
            pltpu.VMEM((ff, rank), bf16),
            pltpu.VMEM((2 * depth, rows, rank), bf16),
            pltpu.VMEM((depth, cut_r, rank), bf16),
            pltpu.VMEM((2 * depth, rows, rank), bf16),
            pltpu.VMEM((2 * depth, rows - cut_r, rank), bf16),
            pltpu.VMEM((rows - cut_r, rank), bf16),
            pltpu.VMEM((2, tokens, rank), f32),
            pltpu.VMEM((2, tokens, rank), f32),
            pltpu.VMEM((tokens, rank), f32),
            pltpu.VMEM((tokens, rank), bf16),
            pltpu.VMEM((rank, width), f32),
            pltpu.VMEM((rank, width), bf16),
            pltpu.VMEM((rank // 2, width), bf16),
            pltpu.VMEM((quarter, width), bf16),
            pltpu.VMEM((quarter, width), bf16),
            pltpu.VMEM((quarter, width), bf16),
            pltpu.VMEM((depth, quarter, chunk), bf16),
            pltpu.VMEM((rank, width), bf16),
            pltpu.VMEM((2, 8, 128), f32),
            pltpu.VMEM((8, 128), f32),
            pltpu.VMEM((8, 128), f32),
            pltpu.VMEM((depth, 8, 128), f32),
            dma((7,)), dma((144,)), dma((2 * n,)),
            dma((2 * depth,)), dma((depth,)), dma((2 * depth,)), dma((2 * depth,)), dma((1,)),
            dma((2,)), dma((depth,)), dma((depth,)), dma((depth,)), dma((n,)),
            dma((2,)), dma((depth,)),
        ],
        compiler_params=pltpu.CompilerParams(
            collective_id=0, has_side_effects=True, vmem_limit_bytes=48 * 1024 * 1024
        ),
        name="fused",
    )(
        *(
            pltpu.with_memory_space_constraint(v, pltpu.HBM)
            for v in (
                activations, output_gradient, adapter_a[0], adapter_b,
                log_ratio.reshape(-1, 128), lengths, rewards,
            )
        )
    )
    grad_a, grad_b, loss = pl.pallas_call(
        finish_kernel,
        out_shape=(
            jax.ShapeDtypeStruct((rows, rank), f32),
            jax.ShapeDtypeStruct((rank, width), f32),
            jax.ShapeDtypeStruct((1, 1), f32),
        ),
        in_specs=[vmem, vmem, vmem],
        out_specs=(hbm, hbm, scalars),
        scratch_shapes=[dma((2,))],
        compiler_params=pltpu.CompilerParams(vmem_limit_bytes=4 * 1024 * 1024),
        name="finish",
    )(grad_a, grad_b, loss)
    return grad_a[None], grad_b, loss.reshape(())


def fits(mesh):
    n, split = mesh.shape["dp"], mesh.shape["tensor"]
    return n % 4 == 0 and 4 <= n <= 16 and split == 2


def local(activations, output_gradient, adapter_a, adapter_b, log_ratio, lengths, rewards):
    n = lax.axis_size("dp")
    rows, rank = adapter_a.shape[1:]
    width, ff = output_gradient.shape[1], activations.shape[1]
    small = 2 * activations.size + 8 * ff * rank < 32 * 1024 * 1024
    aligned = (
        rows % 16 == 0
        and rank == 128
        and activations.shape[0] % 128 == 0
        and ff % 128 == 0
        and 4 * rows % 128 == 0
        and rows >= 64
        and width % (128 * (n // 4)) == 0
        and n % lengths.shape[0] == 0
    )
    run = fused_local if small and aligned else plain_local
    return run(activations, output_gradient, adapter_a, adapter_b, log_ratio, lengths, rewards)


def solution(mesh):
    in_specs = (
        P("dp", "tensor"),
        P("dp", "tensor"),
        P("tensor", "dp", None),
        P(None, "tensor"),
        P("dp"),
        P(),
        P(),
    )
    out_specs = (P("tensor", "dp", None), P(None, "tensor"), P())
    body = local if fits(mesh) else plain_local
    return jax.shard_map(body, mesh=mesh, in_specs=in_specs, out_specs=out_specs, check_vma=False)
```

time: 82 us -> 71.2 us (0.87)
  Pallas kernels: 81.2 us -> 70.4 us
    pallas_call x1, Pallas kernels: 79.5 us -> 68.7 us  [fused_local(): pl.pallas_call(functools.partial(fused_kernel, n, lengths.shape[0], lengt...]
where the time goes in v2:
time: 71.2 us; the launch traced here: 71.1 us
  Pallas kernels  70.4 us (99%)
    pallas_call x1, Pallas kernels, fused_local(): pl.pallas_call(functools.partial(fused_kernel, n, lengths.shape[0], lengt...  68.7 us
    pallas_call x1, Pallas kernels, fused_local(): pl.pallas_call(finish_kernel, out_shape=(jax.ShapeDtypeStruct((rows, rank...  1.74 us

profile of v2, /device:TPU:1, one launch (start us, length us, event | category | flops | bytes accessed | tf_op | source)
XLA Modules:
  0.0 71.1 jit_solution(10587636103131881700)
XLA Ops:
  0.6 68.7 %fused.1 = (f32[864,128]{1,0:T(8,128)S(1)}, f32[128,2560]{1,0:T(8,128)S(1)}, f32[8,128]{1,0:T(8,128)S(1)}) custom-call(bf16[256,13824]{1,0:T(8,128)(2,1)} %act_hbm.1, bf16[256,2560]{1,0:T(8,128)(2,1)} %grad_hbm.1, bf16[864,128]{1,0:T(8,128)(2,1)} %bitcast.4, bf16[128,2560]{1,0:T(8,128)(2,1)} %b_hbm.1, f32[2,128]{1,0:T(2,128)} %bitcast.5, s32[1,16]{1,0:T(1,128)} %len_hbm.1, ...), custom_call_target="tpu_custom_call" | custom-call | tf_op jit(solution)/shard_map/fused/pallas_call | solution.py:557
  69.3 1.7 %finish.1 = (f32[864,128]{1,0:T(8,128)}, f32[128,2560]{1,0:T(8,128)}, f32[1,1]{1,0:T(1,128)}) custom-call(f32[864,128]{1,0:T(8,128)S(1)} %get-tuple-element.9.a_in, f32[128,2560]{1,0:T(8,128)S(1)} %get-tuple-element.10.b_in, f32[8,128]{1,0:T(8,128)S(1)} %get-tuple-element.11.loss_in), custom_call_target="tpu_custom_call" | custom-call | tf_op jit(solution)/shard_map/finish/pallas_call | solution.py:614

commit v3 on v2

--- a/solution.py
+++ b/solution.py
@@ -1,5 +1,6 @@
 import contextlib
 import functools
+import math
 
 import jax
 import jax.numpy as jnp
@@ -97,9 +98,9 @@
     act_hbm, grad_hbm, a_hbm, b_hbm, ratio_hbm, len_hbm, rew_hbm,
     out_a, out_b, out_loss,
     ratio_ref, len_ref, rew_ref,
-    act, grad, b_mat, a_all, part, rs1, rs2, rs3, rs3x, rs4, xs, xr, coef, err,
+    act, grad, b_mat, a_all, part, rs1, rs2, rs3, rs3x, rs4, xs, xr, low_s, low_r, coef, err,
     gb, gbs, gb1, gb2s, gb2, gb3s, gb3, fin, ls, l1, l2, lz,
-    loc, send_s, ag_r, rs1_r, rs2_r, rs3_r, rs3x_r, rs4_r,
+    fac, loc, send_s, ag_r, ag_c, rs1_r, rs2_r, rs3_r, rs3x_r, rs4_r,
     x_r, g1_r, g2_r, g3_r, fin_r, l_r, lz_r,
 ):
     depth = n // 4
@@ -137,53 +138,9 @@
     pl.semaphore_signal(barrier, inc=1, device_id=(p, 1 - t), device_id_type=MESH)
     for copy in [load_a, load_g, load_b] + small + [load_x]:
         copy.start()
-    load_g.wait()
-    load_b.wait()
-    xs[0] = lax.dot_general(grad[...], b_mat[...], (((1,), (1,)), ((), ())), preferred_element_type=f32)
-    for copy in small:
-        copy.wait()
-
-    per_group = n // groups
-    group = p // per_group
-    offset = (p % per_group) * tokens
-    slots = (
-        lax.broadcasted_iota(jnp.int32, ratio_ref.shape, 0) * 128
-        + lax.broadcasted_iota(jnp.int32, ratio_ref.shape, 1)
-        + offset
-    )
-    live_total = jnp.int32(0)
-    live = jnp.zeros(ratio_ref.shape, f32)
-    token_adv = jnp.zeros(ratio_ref.shape, f32)
-    for g in range(groups):
-        here = jnp.full((1, 128), (group == g).astype(f32))
-        reward = [jnp.full((1, 128), rew_ref[g, i]).astype(f32) for i in range(rollouts)]
-        center = sum(reward) / rollouts
-        spread = sum((r - center) * (r - center) for r in reward) / rollouts
-        scale = jnp.sqrt(spread + 1.0)
-        end = jnp.int32(0)
-        for i in range(rollouts):
-            start = end
-            end = end + len_ref[g, i]
-            member = ((slots >= start) & (slots < end)).astype(f32) * here
-            live = live + member
-            token_adv = token_adv + member * ((reward[i] - center) / scale)
-        live_total = live_total + jnp.minimum(end, per_group * tokens)
-    ratio = jnp.exp(ratio_ref[...])
-    unclipped = ratio * token_adv
-    clipped = jnp.clip(ratio, 1.0 - clip_eps, 1.0 + clip_eps) * token_adv
-    token_loss = -jnp.minimum(unclipped, clipped)
-    slope = jnp.where(unclipped <= clipped, -unclipped, jnp.zeros_like(unclipped))
-    weight = live * slope
-    for i in range(tokens // 128):
-        coef[pl.ds(i * 128, 128), :] = jnp.broadcast_to(weight[i : i + 1, :], (128, 128)).T
-    factor = groups / jnp.full((1, 128), live_total).astype(f32)
-    loss_part = jnp.sum(jnp.sum(live * token_loss, axis=1, keepdims=True), axis=0, keepdims=True)
-    ls[0] = jnp.broadcast_to(loss_part, (8, 128))
     load_a.wait()
-    load_x.wait()
     with jax.named_scope("barrier") if SCOPES else contextlib.nullcontext():
         pl.semaphore_wait(barrier, depth + 2)
-
     flip = (2 * z > last).astype(jnp.int32)
     tile = tile_of(4 * rows, 1280)
     steps = 4 * rows // tile
@@ -205,9 +162,16 @@
             return up if k < u else down
 
         def go(s, d, rs, device, tensor=None):
-            copy = remote(s, d, send_s.at[len(sent)], rs, device, tensor)
-            copy.start()
-            sent.append(copy)
+            size = s.dtype.itemsize * math.prod(s.shape) // 256
+            if not sent or sent[-1] + size > ff:
+                sent.append(0)
+            sent[-1] += size
+            remote(s, d, send_s.at[len(sent) - 1], rs, device, tensor).start()
+
+        def drain():
+            for i, size in enumerate(sent):
+                ref = a_all.at[pl.ds(0, size)]
+                remote(ref, ref, send_s.at[i], send_s.at[i], core).wait_send()
 
         def got(d, rs):
             remote(d, d, send_s.at[0], rs, core).wait_recv()
@@ -215,63 +179,87 @@
         def z_dev(k):
             return dev(k, y, c)
 
-        def piece(k, yy, cc, i):
-            q = dev(k, yy, cc)
-            low, size = (0, cut_g) if i == 0 else (cut_g, rows - cut_g)
-            return a_all.at[pl.ds(pl.multiple_of(q * rows + low, 16), size)], ag_r.at[2 * q + i]
+        cuts = [(0, cut_g // 32 * 16), (cut_g // 32 * 16, cut_g), (cut_g, rows)]
+
+        def piece(k, yy, i):
+            low, high = cuts[i]
+            ref = a_all.at[pl.ds(pl.multiple_of(dev(k, yy, c) * rows + low, 16), high - low)]
+            return ref, ag_r.at[(m(k) * 2 + yy) * 3 + i]
 
         def a_send(k, yy, i, *devices):
-            ref, sem = piece(k, yy, c, i)
+            ref, sem = piece(k, yy, i)
             for device in devices:
                 if device is not None:
-                    go(ref, ref, sem, device)
-
-        def a_wait(k, yy, cc, i):
-            got(*piece(k, yy, cc, i))
+                    go(ref, ref, sem if device is not core else ag_c.at[m(k) * 2 + yy], device)
+
+        def a_wait(k, yy, i):
+            got(*piece(k, yy, i))
+
+        def a_core(k, yy):
+            got(
+                a_all.at[pl.ds(pl.multiple_of(dev(k, yy, 1 - c) * rows, 16), rows)],
+                ag_c.at[m(k) * 2 + yy],
+            )
 
         up_dev = None if up is None else z_dev(up)
         down_dev = None if down is None else z_dev(down)
 
         def a_start():
             a_send(u, y, 0, up_dev, down_dev)
-            a_send(u, y, 1, side, up_dev, down_dev)
+            a_send(u, y, 2, side)
+            a_send(u, y, 1, up_dev, down_dev)
+            a_send(u, y, 2, up_dev, down_dev)
             a_send(u, y, 0, side)
-            a_send(u, y, 0, core)
-            a_send(u, y, 1, core)
+            a_send(u, y, 1, side)
+            for i in range(3):
+                a_send(u, y, i, core)
 
         def a_side(i):
-            a_wait(u, 1 - y, c, i)
-            if i == 1:
-                a_send(u, 1 - y, 1, up_dev, down_dev)
+            a_wait(u, 1 - y, i)
+            if i == 2:
+                a_send(u, 1 - y, i, up_dev, down_dev)
             a_send(u, 1 - y, i, core)
 
         def a_line(k, yy, i):
-            a_wait(k, yy, c, i)
+            a_wait(k, yy, i)
             to = onward(k)
             a_send(k, yy, i, None if to is None else z_dev(to))
-            if i == 0:
+            if i < 2:
                 a_send(k, yy, i, side)
             a_send(k, yy, i, core)
 
-        def a_over(k):
-            a_wait(k, 1 - y, c, 0)
-            a_send(k, 1 - y, 0, core)
+        def a_over(k, i):
+            a_wait(k, 1 - y, i)
+            a_send(k, 1 - y, i, core)
+
+        def low_rows(start, size, first=False):
+            width_of = size if size <= 2048 else tile_of(size, 1280)
+
+            def step(i, total):
+                cols = pl.ds(pl.multiple_of(start + i * width_of, 128), width_of)
+                return total + jnp.dot(act[:, cols], a_all[cols, :], preferred_element_type=f32)
+
+            begin = jnp.zeros((tokens, rank), f32) if first else xs[1]
+            xs[1] = lax.fori_loop(0, size // width_of, step, begin)
 
         def low_of(k, first):
             for yy in (0, 1):
-                for i in (0, 1):
-                    a_wait(k, yy, 1 - c, i)
-            base = m(k) * (4 * rows)
-
-            def step(i, total):
-                cols = pl.ds(pl.multiple_of(base + i * tile, 128), tile)
-                return total + jnp.dot(act[:, cols], a_all[cols, :], preferred_element_type=f32)
-
-            begin = jnp.zeros((tokens, rank), f32) if first else xs[1]
-            xs[1] = lax.fori_loop(0, steps, step, begin)
+                a_core(k, yy)
+            low_rows(m(k) * (4 * rows), 4 * rows, first)
+
+        small_part = 2 * rows // 128 * 128
+
+        def low_near(k):
+            a_core(k, y)
+            low_rows(m(k) * (4 * rows) + y * (4 * rows - small_part), small_part)
+
+        def low_far(k):
+            a_core(k, 1 - y)
+            low_rows(m(k) * (4 * rows) + (1 - y) * small_part, 4 * rows - small_part)
 
         def low_send():
-            go(xs.at[1], xr.at[1], x_r.at[1], p, 1 - t)
+            low_s[...] = xs[1].astype(bf16)
+            go(low_s, low_r, x_r.at[1], p, 1 - t)
 
         def loss_one():
             go(ls.at[0], l1, l_r.at[0], core)
@@ -293,14 +281,59 @@
             total = lz[0]
             for i in range(1, depth):
                 total = total + lz[i]
-            out_loss[...] = factor * total
+            out_loss[...] = fac[...] * total
 
         def back_send():
-            go(xs.at[0], xr.at[0], x_r.at[0], p, 1 - t)
+            load_g.wait()
+            load_b.wait()
+            xs[0] = lax.dot_general(
+                grad[...], b_mat[...], (((1,), (1,)), ((), ())), preferred_element_type=f32
+            )
+            go(xs.at[0], xr, x_r.at[0], p, 1 - t)
+
+        def token_terms_here():
+            for copy in small:
+                copy.wait()
+            per_group = n // groups
+            group = p // per_group
+            offset = (p % per_group) * tokens
+            slots = (
+                lax.broadcasted_iota(jnp.int32, ratio_ref.shape, 0) * 128
+                + lax.broadcasted_iota(jnp.int32, ratio_ref.shape, 1)
+                + offset
+            )
+            live_total = jnp.int32(0)
+            live = jnp.zeros(ratio_ref.shape, f32)
+            token_adv = jnp.zeros(ratio_ref.shape, f32)
+            for g in range(groups):
+                here = jnp.full((1, 128), (group == g).astype(f32))
+                reward = [jnp.full((1, 128), rew_ref[g, i]).astype(f32) for i in range(rollouts)]
+                center = sum(reward) / rollouts
+                spread = sum((r - center) * (r - center) for r in reward) / rollouts
+                scale = jnp.sqrt(spread + 1.0)
+                end = jnp.int32(0)
+                for i in range(rollouts):
+                    start = end
+                    end = end + len_ref[g, i]
+                    member = ((slots >= start) & (slots < end)).astype(f32) * here
+                    live = live + member
+                    token_adv = token_adv + member * ((reward[i] - center) / scale)
+                live_total = live_total + jnp.minimum(end, per_group * tokens)
+            ratio = jnp.exp(ratio_ref[...])
+            unclipped = ratio * token_adv
+            clipped = jnp.clip(ratio, 1.0 - clip_eps, 1.0 + clip_eps) * token_adv
+            token_loss = -jnp.minimum(unclipped, clipped)
+            slope = jnp.where(unclipped <= clipped, -unclipped, jnp.zeros_like(unclipped))
+            weight = live * slope
+            for i in range(tokens // 128):
+                coef[pl.ds(i * 128, 128), :] = jnp.broadcast_to(weight[i : i + 1, :], (128, 128)).T
+            fac[...] = groups / jnp.full((1, 128), live_total).astype(f32)
+            loss_part = jnp.sum(jnp.sum(live * token_loss, axis=1, keepdims=True), axis=0, keepdims=True)
+            ls[0] = jnp.broadcast_to(loss_part, (8, 128))
 
         def back_end():
-            got(xr.at[0], x_r.at[0])
-            err[...] = (adapter_scale_factor * coef[...] * (xs[0] + xr[0])).astype(bf16)
+            got(xr, x_r.at[0])
+            err[...] = (adapter_scale_factor * coef[...] * (xs[0] + xr[...])).astype(bf16)
 
         def span(k, yy, cc, part_two=None):
             q = dev(k, yy, cc)
@@ -320,16 +353,16 @@
             lax.fori_loop(0, steps, step, 0)
             for yy in (1 - y, y):
                 slot = m(k) * 2 + yy
-                go(span(k, yy, 1 - c), rs1.at[slot], rs1_r.at[slot], core)
+                go(span(k, yy, 1 - c), rs1.at[slot], rs1_r.at[m(k)], core)
 
         def both(k, yy, i):
             low, size = (0, cut_r) if i == 0 else (cut_r, rows - cut_r)
             return span(k, yy, c, i)[...].astype(f32) + rs1[m(k) * 2 + yy, pl.ds(low, size), :].astype(f32)
 
+        def core_wait(k):
+            got(rs1.at[pl.ds(m(k) * 2, 2)], rs1_r.at[m(k)])
+
         def core_sum(k):
-            for yy in (1 - y, y):
-                slot = m(k) * 2 + yy
-                got(rs1.at[slot], rs1_r.at[slot])
             ref = span(k, 1 - y, c, 0)
             ref[...] = both(k, 1 - y, 0).astype(bf16)
             go(ref, rs2.at[m(k)], rs2_r.at[m(k)], side)
@@ -346,43 +379,40 @@
             return found
 
         def line_x(k):
-            total = both(k, 1 - y, 1)
+            for b, yy in enumerate((1 - y, y)):
+                total = both(k, yy, 1)
+                for slot in sources(k):
+                    got(rs3x.at[b, slot], rs3x_r.at[b, slot])
+                    total = total + rs3x[b, slot].astype(f32)
+                ref = span(k, yy, c, 1)
+                if k != u:
+                    ref[...] = total.astype(bf16)
+                    slot = line_slot(k, k > u)
+                    go(ref, rs3x.at[b, slot], rs3x_r.at[b, slot], z_dev(up if k > u else down))
+                elif b == 0:
+                    ref[...] = total.astype(bf16)
+                    go(ref, rs4, rs4_r.at[0], side)
+                else:
+                    out_a[pl.ds(cut_r, rows - cut_r), :] = total
+
+        def line_sum(k):
+            got(rs2.at[m(k)], rs2_r.at[m(k)])
+            total = both(k, y, 0) + rs2[m(k)].astype(f32)
             for slot in sources(k):
-                got(rs3x.at[slot], rs3x_r.at[slot])
-                total = total + rs3x[slot].astype(f32)
-            ref = span(k, 1 - y, c, 1)
-            ref[...] = total.astype(bf16)
+                got(rs3.at[slot], rs3_r.at[slot])
+                total = total + rs3[slot].astype(f32)
             if k == u:
-                go(ref, rs4, rs4_r.at[0], side)
-            else:
-                slot = line_slot(k, k > u)
-                go(ref, rs3x.at[slot], rs3x_r.at[slot], z_dev(up if k > u else down))
-
-        def line_sum(k):
-            slots_in = sources(k)
-            got(rs2.at[m(k)], rs2_r.at[m(k)])
-            for slot in slots_in:
-                got(rs3.at[slot], rs3_r.at[slot])
-            first = both(k, y, 0) + rs2[m(k)].astype(f32)
-            second = both(k, y, 1)
-            for slot in slots_in:
-                first = first + rs3[slot, pl.ds(0, cut_r), :].astype(f32)
-                second = second + rs3[slot, pl.ds(cut_r, rows - cut_r), :].astype(f32)
-            if k == u:
-                out_a[pl.ds(0, cut_r), :] = factor * first
-                out_a[pl.ds(cut_r, rows - cut_r), :] = second
+                out_a[pl.ds(0, cut_r), :] = fac[...] * total
             else:
                 ref = span(k, y, c, 0)
-                ref[...] = first.astype(bf16)
-                ref = span(k, y, c, 1)
-                ref[...] = second.astype(bf16)
+                ref[...] = total.astype(bf16)
                 slot = line_slot(k, k > u)
-                go(span(k, y, c), rs3.at[slot], rs3_r.at[slot], z_dev(up if k > u else down))
+                go(ref, rs3.at[slot], rs3_r.at[slot], z_dev(up if k > u else down))
 
         def a_end():
             got(rs4, rs4_r.at[0])
             rest = pl.ds(cut_r, rows - cut_r)
-            out_a[rest, :] = factor * (out_a[rest, :] + rs4[...].astype(f32))
+            out_a[rest, :] = fac[...] * (out_a[rest, :] + rs4[...].astype(f32))
 
         lane = pl.multiple_of(c * half, 16)
         other = pl.multiple_of((1 - c) * half, 16)
@@ -395,17 +425,15 @@
             return pl.ds(pl.multiple_of(m(k) * chunk, 128), chunk)
 
         def b_part():
-            got(xr.at[1], x_r.at[1])
-            weighted = coef[...] * (xs[1] + xr[1])
+            got(low_r, x_r.at[1])
+            weighted = coef[...] * (xs[1] + low_r[...].astype(f32))
             high = weighted.astype(bf16)
-            rest = weighted - high.astype(f32)
-            middle = rest.astype(bf16)
-            last_part = (rest - middle.astype(f32)).astype(bf16)
+            rest = (weighted - high.astype(f32)).astype(bf16)
             for k in b_order:
                 cols = cols_of(k)
                 total = sum(
                     lax.dot_general(w, grad[:, cols], (((0,), (0,)), ((), ())), preferred_element_type=f32)
-                    for w in (last_part, middle, high)
+                    for w in (rest, high)
                 )
                 gb[:, cols] = total
                 gbs[:, cols] = total.astype(bf16)
@@ -436,12 +464,12 @@
 
         def final(k, yy, cc):
             at_row = pl.multiple_of(cc * half + yy * quarter, 16)
-            return fin.at[pl.ds(at_row, quarter), cols_of(k)], fin_r.at[dev(k, yy, cc)]
+            return fin.at[pl.ds(at_row, quarter), cols_of(k)], fin_r.at[m(k) * 2 + yy]
 
         def b_send(k, yy, *devices):
             ref, sem = final(k, yy, c)
             for device in devices:
-                go(ref, ref, sem, device)
+                go(ref, ref, sem if device is not core else fin_r.at[2 * depth], device)
 
         def b_line():
             cols = cols_of(u)
@@ -449,7 +477,7 @@
             for k in others:
                 got(gb3.at[m(k)], g3_r.at[m(k)])
                 total = total + gb3[m(k)].astype(f32)
-            scaled = jnp.full((1, 128), adapter_scale_factor) * factor
+            scaled = jnp.full((1, 128), adapter_scale_factor) * fac[...]
             fin[pl.ds(mine, quarter), cols] = (scaled[:, :1] * total).astype(bf16)
             b_send(u, y, *[z_dev(k) for k in others[::-1]], side, core)
 
@@ -460,69 +488,87 @@
             b_send(k, yy, core)
 
         def b_end():
-            for k in [u] + others:
-                for yy in (y, 1 - y):
-                    got(*final(k, yy, 1 - c))
+            got(fin.at[pl.ds(other, half)], fin_r.at[2 * depth])
             out_b[...] = fin[...].astype(f32)
 
         there = 1 - y
         plan = [
-            (0.0, a_start), (0.1, back_send), (0.2, loss_one),
-            (3.0, a_side, 1), (4.5, back_end), (6.4, a_side, 0), (7.2, loss_two), (9.5, loss_three),
+            (0.0, a_start), (0.1, back_send), (0.2, token_terms_here), (0.3, loss_one), (0.4, load_x.wait),
+            (2.9, a_side, 2), (4.55, back_end), (4.7, a_side, 0), (6.4, a_side, 1), (7.2, loss_two), (21.5, loss_three),
         ]
         order = [k for k in (range(last, -1, -1)) if k > u] + [k for k in range(u)] + [u]
         for i, k in enumerate(order):
-            plan.append((4.6 + 0.95 * i, part_of, k))
-            plan.append((7.05 + 0.95 * i, core_sum, k))
+            plan.append((4.6 + 1.1 * i, part_of, k))
+            plan.append((8.0 + 1.15 * i, core_wait, k))
+            first = 17.35 if u == 0 else 11.35
+            plan.append((max(first, 8.0 + 1.15 * i) + 0.01 * (i + 1), core_sum, k))
         if u == 0:
             for i, k in enumerate(order[:-1]):
-                plan.append(((7.1, 8.1, 12.0)[i % 3], line_x, k))
-                plan.append(((11.0, 13.0, 14.0)[i % 3], line_sum, k))
-            plan.append((22.0, line_x, u))
-            plan.append((30.0, line_sum, u))
+                plan.append((8.05 + 1.15 * i, line_x, k))
         else:
             for k in order:
                 if k > u:
-                    plan.append((11.5 + 2.0 * (last - k), line_x, k))
-                    plan.append((17.0 + 5.0 * (last - k), line_sum, k))
+                    plan.append((15.1 + 4.8 * (last - k), line_x, k))
+                    plan.append((28.5 + 2.5 * (last - k), line_sum, k))
                 elif k < u:
-                    plan.append((16.0, line_x, k))
-                    plan.append((23.5, line_sum, k))
+                    plan.append((21.7, line_x, k))
+                    plan.append((33.0, line_sum, k))
                 else:
-                    plan.append((20.0, line_x, k))
-                    plan.append((30.0, line_sum, k))
-        plan.append((31.0, a_end))
+                    plan.append((26.6, line_x, k))
         when = {}
         for k in others:
             hops = abs(k - u)
-            when[k] = 5.2 + 6.0 * (hops - 1)
+            when[k] = 3.5 + 6.0 * (hops - 1)
             plan.append((when[k], a_line, k, y, 0))
-            plan.append((when[k] + 1.2, a_line, k, y, 1))
-            plan.append((when[k] + 2.5, a_line, k, there, 1))
-            plan.append((when[k] + 5.2, a_over, k))
+            plan.append((when[k] + 1.7, a_line, k, y, 1))
+            plan.append((when[k] + 2.9, a_line, k, y, 2))
+            plan.append((when[k] + 4.2, a_line, k, there, 2))
+        queue = 4.7
+        for i in (0, 1):
+            for k in others:
+                if u == 0 or abs(k - u) == 1:
+                    queue = max(queue, when[k] + 1.7 * i) + 1.75 if u else when[k] + 1.7 * i + 1.75
+                    when[k, i] = queue + (1.8 if u else 3.3)
+                    plan.append((when[k, i], a_over, k, i))
+        for i in (0, 1):
+            for k in others:
+                if u > 0 and abs(k - u) > 1:
+                    queue = max(queue, when[k] + 1.7 * i) + 1.75
+                    when[k, i] = queue + (1.8 if u else 3.3)
+                    plan.append((when[k, i], a_over, k, i))
         for i, k in enumerate([u] + others):
-            done = 9.0 if i == 0 else when[k] + 6.4 + 0.1 * i
-            plan.append((done, low_of, k, i == 0))
+            done = 9.0 if i == 0 else when[k, 1] + 1.2 + 0.1 * i
+            if i < depth - 1 or depth == 1:
+                plan.append((done, low_of, k, i == 0))
+            else:
+                plan.append((done - 0.6, low_near, k))
+                plan.append((done, low_far, k))
         plan.append((done + 0.1, low_send))
-        begin = done + 5.0
+        begin = done + 4.5
+        if u == 0:
+            plan.append((begin + 1.6, line_x, u))
+            for k, moment in zip(order[:-1], (done + 0.15, done + 0.3, begin + 1.55)):
+                plan.append((moment, line_sum, k))
         plan.append((begin, b_part))
         for i, k in enumerate(b_order):
             plan.append((begin + 1.5 + 0.01 * i, b_core, k))
             plan.append((begin + 4.5 + 0.9 * i, b_side, k))
-        begin = 6.0 * last + 10.6 + 0.1 * last
+        begin = max(begin, 6.0 * last + 10.3)
         plan.append((begin + 9.5, b_line))
-        plan.append((begin + 11.5, b_pass, u, there))
+        plan.append((begin + 13.9, line_sum, u))
+        plan.append((begin + 13.91, a_end))
+        plan.append((begin + 15.5, b_pass, u, there))
         for i, k in enumerate(others):
             plan.append((begin + 12.0 + 0.9 * i, b_pass, k, y))
             plan.append((begin + 14.0 + 0.9 * i, b_pass, k, there))
         plan.append((begin + 18.0, loss_end))
         plan.append((begin + 19.0, b_end))
         for entry in sorted(plan, key=lambda e: e[0]):
-            name = entry[1].__name__ + "_".join(str(v) for v in entry[2:] if isinstance(v, int))
+            name = getattr(entry[1], "__name__", "w") + "_".join(str(v) for v in entry[2:] if isinstance(v, int))
             with jax.named_scope(name) if SCOPES else contextlib.nullcontext():
                 entry[1](*entry[2:])
-        for copy in sent:
-            copy.wait_send()
+        with jax.named_scope("drain") if SCOPES else contextlib.nullcontext():
+            drain()
 
     for u in range((depth + 1) // 2):
         @pl.when(jnp.minimum(z, last - z) == u)
@@ -574,11 +620,13 @@
             pltpu.VMEM((ff, rank), bf16),
             pltpu.VMEM((2 * depth, rows, rank), bf16),
             pltpu.VMEM((depth, cut_r, rank), bf16),
-            pltpu.VMEM((2 * depth, rows, rank), bf16),
-            pltpu.VMEM((2 * depth, rows - cut_r, rank), bf16),
+            pltpu.VMEM((2 * depth, cut_r, rank), bf16),
+            pltpu.VMEM((2, 2 * depth, rows - cut_r, rank), bf16),
             pltpu.VMEM((rows - cut_r, rank), bf16),
             pltpu.VMEM((2, tokens, rank), f32),
-            pltpu.VMEM((2, tokens, rank), f32),
+            pltpu.VMEM((tokens, rank), f32),
+            pltpu.VMEM((tokens, rank), bf16),
+            pltpu.VMEM((tokens, rank), bf16),
             pltpu.VMEM((tokens, rank), f32),
             pltpu.VMEM((tokens, rank), bf16),
             pltpu.VMEM((rank, width), f32),
@@ -593,9 +641,10 @@
             pltpu.VMEM((8, 128), f32),
             pltpu.VMEM((8, 128), f32),
             pltpu.VMEM((depth, 8, 128), f32),
-            dma((7,)), dma((144,)), dma((2 * n,)),
-            dma((2 * depth,)), dma((depth,)), dma((2 * depth,)), dma((2 * depth,)), dma((1,)),
-            dma((2,)), dma((depth,)), dma((depth,)), dma((depth,)), dma((n,)),
+            pltpu.VMEM((1, 128), f32),
+            dma((7,)), dma((4,)), dma((6 * depth,)), dma((2 * depth,)),
+            dma((depth,)), dma((depth,)), dma((2 * depth,)), dma((2, 2 * depth)), dma((1,)),
+            dma((2,)), dma((depth,)), dma((depth,)), dma((depth,)), dma((2 * depth + 1,)),
             dma((2,)), dma((depth,)),
         ],
         compiler_params=pltpu.CompilerParams(

time: 71.2 us -> 55.6 us (0.78)
  Pallas kernels: 70.4 us -> 54.8 us
    pallas_call x1, Pallas kernels: 68.7 us -> 53 us  [fused_local(): pl.pallas_call(functools.partial(fused_kernel, n, lengths.shape[0], lengt...]
where the time goes in v3:
time: 55.6 us; the launch traced here: 55.4 us
  Pallas kernels  54.8 us (99%)
  between operations  0.64 us (1%)
    pallas_call x1, Pallas kernels, fused_local(): pl.pallas_call(functools.partial(fused_kernel, n, lengths.shape[0], lengt...  53 us
    pallas_call x1, Pallas kernels, fused_local(): pl.pallas_call(finish_kernel, out_shape=(jax.ShapeDtypeStruct((rows, rank...  1.74 us

profile of v3, /device:TPU:1, one launch (start us, length us, event | category | flops | bytes accessed | tf_op | source)
XLA Modules:
  0.0 55.4 jit_solution(1215425962283928745)
XLA Ops:
  0.6 53.0 %fused.1 = (f32[864,128]{1,0:T(8,128)S(1)}, f32[128,2560]{1,0:T(8,128)S(1)}, f32[8,128]{1,0:T(8,128)S(1)}) custom-call(bf16[256,13824]{1,0:T(8,128)(2,1)} %act_hbm.1, bf16[256,2560]{1,0:T(8,128)(2,1)} %grad_hbm.1, bf16[864,128]{1,0:T(8,128)(2,1)} %bitcast.4, bf16[128,2560]{1,0:T(8,128)(2,1)} %b_hbm.1, f32[2,128]{1,0:T(2,128)} %bitcast.5, s32[1,16]{1,0:T(1,128)} %len_hbm.1, ...), custom_call_target="tpu_custom_call" | custom-call | tf_op jit(solution)/shard_map/fused/pallas_call | solution.py:603
  53.7 1.7 %finish.1 = (f32[864,128]{1,0:T(8,128)}, f32[128,2560]{1,0:T(8,128)}, f32[1,1]{1,0:T(1,128)}) custom-call(f32[864,128]{1,0:T(8,128)S(1)} %get-tuple-element.9.a_in, f32[128,2560]{1,0:T(8,128)S(1)} %get-tuple-element.10.b_in, f32[8,128]{1,0:T(8,128)S(1)} %get-tuple-element.11.loss_in), custom_call_target="tpu_custom_call" | custom-call | tf_op jit(solution)/shard_map/finish/pallas_call | solution.py:663

commit v4 on v3

--- a/solution.py
+++ b/solution.py
@@ -98,7 +98,7 @@
     act_hbm, grad_hbm, a_hbm, b_hbm, ratio_hbm, len_hbm, rew_hbm,
     out_a, out_b, out_loss,
     ratio_ref, len_ref, rew_ref,
-    act, grad, b_mat, a_all, part, rs1, rs2, rs3, rs3x, rs4, xs, xr, low_s, low_r, coef, err,
+    act, grad, b_mat, a_all, part, rs1, rs2, rs3, rs3x, rs4, xs, back_s, back_r, low_s, low_r, coef, err,
     gb, gbs, gb1, gb2s, gb2, gb3s, gb3, fin, ls, l1, l2, lz,
     fac, loc, send_s, ag_r, ag_c, rs1_r, rs2_r, rs3_r, rs3x_r, rs4_r,
     x_r, g1_r, g2_r, g3_r, fin_r, l_r, lz_r,
@@ -111,7 +111,7 @@
     tokens, ff = act.shape
     rows, rank = a_hbm.shape
     width = grad.shape[1]
-    half, quarter, chunk = rank // 2, rank // 4, width // depth
+    chunk = width // depth
 
     def at(zz, yy, cc):
         return (zz * 2 + yy) * 2 + cc
@@ -145,8 +145,9 @@
     tile = tile_of(4 * rows, 1280)
     steps = 4 * rows // tile
 
-    def run(u):
+    def run(u, own):
         sent = []
+        mate = 1 - own
 
         def m(k):
             return k + flip * (last - 2 * k)
@@ -154,6 +155,7 @@
         def dev(k, yy, cc):
             return at(m(k), yy, cc)
 
+        there = 1 - y
         others = sorted((k for k in range(depth) if k != u), key=lambda k: abs(k - u))
         up = u + 1 if u < last else None
         down = u - 1 if u > 0 else None
@@ -179,12 +181,17 @@
         def z_dev(k):
             return dev(k, y, c)
 
-        cuts = [(0, cut_g // 32 * 16), (cut_g // 32 * 16, cut_g), (cut_g, rows)]
+        middle = cut_g // 32 * 16
+        first_rows = [(0, middle), (middle, cut_g)]
+        carried = [(own, low, high, True) for low, high in first_rows]
+        if own == 1:
+            carried += [(cc, cut_g, rows, False) for cc in (1, 0)]
+
+        def rows_of(k, yy, cc, low, high):
+            return a_all.at[pl.ds(pl.multiple_of(dev(k, yy, cc) * rows + low, 16), high - low)]
 
         def piece(k, yy, i):
-            low, high = cuts[i]
-            ref = a_all.at[pl.ds(pl.multiple_of(dev(k, yy, c) * rows + low, 16), high - low)]
-            return ref, ag_r.at[(m(k) * 2 + yy) * 3 + i]
+            return rows_of(k, yy, *carried[i][:3]), ag_r.at[(m(k) * 2 + yy) * 4 + i]
 
         def a_send(k, yy, i, *devices):
             ref, sem = piece(k, yy, i)
@@ -196,35 +203,47 @@
             got(*piece(k, yy, i))
 
         def a_core(k, yy):
-            got(
-                a_all.at[pl.ds(pl.multiple_of(dev(k, yy, 1 - c) * rows, 16), rows)],
-                ag_c.at[m(k) * 2 + yy],
-            )
+            size = cut_g
+            if own == 0:
+                size = rows if k == u and yy is y else 2 * rows - cut_g
+            got(a_all.at[pl.ds(0, size)], ag_c.at[m(k) * 2 + yy])
 
         up_dev = None if up is None else z_dev(up)
         down_dev = None if down is None else z_dev(down)
+        line = (up_dev, down_dev)
 
         def a_start():
-            a_send(u, y, 0, up_dev, down_dev)
-            a_send(u, y, 2, side)
-            a_send(u, y, 1, up_dev, down_dev)
-            a_send(u, y, 2, up_dev, down_dev)
+            a_send(u, y, 0, *line)
+            if own == 0:
+                ref = rows_of(u, y, 0, cut_g, rows)
+                go(ref, ref, ag_c.at[2 * depth], core)
+                a_send(u, y, 1, *line)
+                a_send(u, y, 0, side)
+                a_send(u, y, 1, side)
+            else:
+                a_send(u, y, 2, side)
+                a_send(u, y, 1, *line)
+                a_send(u, y, 2, *line)
+            for i in range(2 + own):
+                a_send(u, y, i, core)
+
+        def a_mate():
+            got(rows_of(u, y, 0, cut_g, rows), ag_c.at[2 * depth])
+            a_send(u, y, 3, side, *line)
             a_send(u, y, 0, side)
             a_send(u, y, 1, side)
-            for i in range(3):
-                a_send(u, y, i, core)
 
         def a_side(i):
             a_wait(u, 1 - y, i)
-            if i == 2:
-                a_send(u, 1 - y, i, up_dev, down_dev)
+            if not carried[i][3]:
+                a_send(u, 1 - y, i, *line)
             a_send(u, 1 - y, i, core)
 
         def a_line(k, yy, i):
             a_wait(k, yy, i)
             to = onward(k)
             a_send(k, yy, i, None if to is None else z_dev(to))
-            if i < 2:
+            if carried[i][3]:
                 a_send(k, yy, i, side)
             a_send(k, yy, i, core)
 
@@ -243,7 +262,7 @@
             xs[1] = lax.fori_loop(0, size // width_of, step, begin)
 
         def low_of(k, first):
-            for yy in (0, 1):
+            for yy in (y, there):
                 a_core(k, yy)
             low_rows(m(k) * (4 * rows), 4 * rows, first)
 
@@ -289,7 +308,8 @@
             xs[0] = lax.dot_general(
                 grad[...], b_mat[...], (((1,), (1,)), ((), ())), preferred_element_type=f32
             )
-            go(xs.at[0], xr, x_r.at[0], p, 1 - t)
+            back_s[...] = xs[0].astype(bf16)
+            go(back_s, back_r, x_r.at[0], p, 1 - t)
 
         def token_terms_here():
             for copy in small:
@@ -332,8 +352,8 @@
             ls[0] = jnp.broadcast_to(loss_part, (8, 128))
 
         def back_end():
-            got(xr, x_r.at[0])
-            err[...] = (adapter_scale_factor * coef[...] * (xs[0] + xr[...])).astype(bf16)
+            got(back_r, x_r.at[0])
+            err[...] = (adapter_scale_factor * coef[...] * (xs[0] + back_r[...].astype(f32))).astype(bf16)
 
         def span(k, yy, cc, part_two=None):
             q = dev(k, yy, cc)
@@ -379,16 +399,17 @@
             return found
 
         def line_x(k):
+            for slot in sources(k):
+                got(rs3x.at[slot], rs3x_r.at[slot])
             for b, yy in enumerate((1 - y, y)):
                 total = both(k, yy, 1)
                 for slot in sources(k):
-                    got(rs3x.at[b, slot], rs3x_r.at[b, slot])
-                    total = total + rs3x[b, slot].astype(f32)
+                    total = total + rs3x[slot, b].astype(f32)
                 ref = span(k, yy, c, 1)
                 if k != u:
                     ref[...] = total.astype(bf16)
                     slot = line_slot(k, k > u)
-                    go(ref, rs3x.at[b, slot], rs3x_r.at[b, slot], z_dev(up if k > u else down))
+                    go(ref, rs3x.at[slot, b], rs3x_r.at[slot], z_dev(up if k > u else down))
                 elif b == 0:
                     ref[...] = total.astype(bf16)
                     go(ref, rs4, rs4_r.at[0], side)
@@ -414,8 +435,9 @@
             rest = pl.ds(cut_r, rows - cut_r)
             out_a[rest, :] = fac[...] * (out_a[rest, :] + rs4[...].astype(f32))
 
-        lane = pl.multiple_of(c * half, 16)
-        other = pl.multiple_of((1 - c) * half, 16)
+        bases, halves, quarters = (0, rank // 4), (rank // 4, rank * 3 // 4), (rank // 8, rank * 3 // 8)
+        lane, other, quarter = bases[own], bases[mate], quarters[own]
+        whole = pl.ds(0, quarter)
         away = pl.multiple_of((1 - y) * quarter, 16)
         stay = pl.multiple_of(y * quarter, 16)
         mine = pl.multiple_of(lane + stay, 16)
@@ -437,37 +459,38 @@
                 )
                 gb[:, cols] = total
                 gbs[:, cols] = total.astype(bf16)
-                go(gbs.at[pl.ds(other, half), cols], gb1.at[:, cols], g1_r.at[m(k)], core)
+                rest_rows = pl.ds(0, halves[mate])
+                go(gbs.at[pl.ds(other, halves[mate]), cols], gb1.at[rest_rows, cols], g1_r.at[m(k)], core)
 
         def b_core(k):
             cols = cols_of(k)
-            got(gb1.at[:, cols], g1_r.at[m(k)])
-            gb2s[:, cols] = (
+            got(gb1.at[pl.ds(0, halves[own]), cols], g1_r.at[m(k)])
+            gb2s[whole, cols] = (
                 gb[pl.ds(pl.multiple_of(lane + away, 16), quarter), cols]
                 + gb1[pl.ds(away, quarter), cols].astype(f32)
             ).astype(bf16)
-            go(gb2s.at[:, cols], gb2.at[:, cols], g2_r.at[m(k)], side)
+            go(gb2s.at[whole, cols], gb2.at[whole, cols], g2_r.at[m(k)], side)
 
         def b_side(k):
             cols = cols_of(k)
-            got(gb2.at[:, cols], g2_r.at[m(k)])
+            got(gb2.at[whole, cols], g2_r.at[m(k)])
             total = (
                 gb[pl.ds(mine, quarter), cols]
                 + gb1[pl.ds(stay, quarter), cols].astype(f32)
-                + gb2[:, cols].astype(f32)
+                + gb2[whole, cols].astype(f32)
             )
             if k == u:
                 gb[pl.ds(mine, quarter), cols] = total
             else:
-                gb3s[:, cols] = total.astype(bf16)
-                go(gb3s.at[:, cols], gb3.at[z], g3_r.at[z], z_dev(k))
+                gb3s[whole, cols] = total.astype(bf16)
+                go(gb3s.at[whole, cols], gb3.at[z, whole], g3_r.at[z], z_dev(k))
 
         def final(k, yy, cc):
-            at_row = pl.multiple_of(cc * half + yy * quarter, 16)
-            return fin.at[pl.ds(at_row, quarter), cols_of(k)], fin_r.at[m(k) * 2 + yy]
+            at_row = pl.multiple_of(bases[cc] + yy * quarters[cc], 16)
+            return fin.at[pl.ds(at_row, quarters[cc]), cols_of(k)], fin_r.at[m(k) * 2 + yy]
 
         def b_send(k, yy, *devices):
-            ref, sem = final(k, yy, c)
+            ref, sem = final(k, yy, own)
             for device in devices:
                 go(ref, ref, sem if device is not core else fin_r.at[2 * depth], device)
 
@@ -475,67 +498,72 @@
             cols = cols_of(u)
             total = gb[pl.ds(mine, quarter), cols]
             for k in others:
-                got(gb3.at[m(k)], g3_r.at[m(k)])
-                total = total + gb3[m(k)].astype(f32)
+                got(gb3.at[m(k), whole], g3_r.at[m(k)])
+                total = total + gb3[m(k), whole, :].astype(f32)
             scaled = jnp.full((1, 128), adapter_scale_factor) * fac[...]
             fin[pl.ds(mine, quarter), cols] = (scaled[:, :1] * total).astype(bf16)
             b_send(u, y, *[z_dev(k) for k in others[::-1]], side, core)
 
         def b_pass(k, yy):
-            got(*final(k, yy, c))
-            if yy is y:
+            got(*final(k, yy, own))
+            if yy is y and abs(k - u) > 1:
                 b_send(k, yy, side)
+            if k == u:
+                b_send(k, yy, *[device for device in (up_dev, down_dev) if device is not None])
             b_send(k, yy, core)
 
         def b_end():
-            got(fin.at[pl.ds(other, half)], fin_r.at[2 * depth])
+            got(fin.at[pl.ds(other, halves[mate])], fin_r.at[2 * depth])
             out_b[...] = fin[...].astype(f32)
 
-        there = 1 - y
         plan = [
             (0.0, a_start), (0.1, back_send), (0.2, token_terms_here), (0.3, loss_one), (0.4, load_x.wait),
-            (2.9, a_side, 2), (4.55, back_end), (4.7, a_side, 0), (6.4, a_side, 1), (7.2, loss_two), (21.5, loss_three),
+            (4.55, back_end), (7.2, loss_two), (21.5, loss_three),
         ]
         order = [k for k in (range(last, -1, -1)) if k > u] + [k for k in range(u)] + [u]
         for i, k in enumerate(order):
             plan.append((4.6 + 1.1 * i, part_of, k))
-            plan.append((8.0 + 1.15 * i, core_wait, k))
-            first = 17.35 if u == 0 else 11.35
-            plan.append((max(first, 8.0 + 1.15 * i) + 0.01 * (i + 1), core_sum, k))
+            ready = 7.3 + 1.15 * i
+            plan.append((ready, core_wait, k))
+            first = ready if i == 0 else (17.35 if u == 0 else 11.35)
+            plan.append((max(first, ready) + 0.01 * (i + 1), core_sum, k))
         if u == 0:
             for i, k in enumerate(order[:-1]):
-                plan.append((8.05 + 1.15 * i, line_x, k))
+                plan.append((7.35 + 1.15 * i if i < 2 else 15.4, line_x, k))
+            plan.append((15.3, line_sum, order[0]))
         else:
             for k in order:
                 if k > u:
                     plan.append((15.1 + 4.8 * (last - k), line_x, k))
-                    plan.append((28.5 + 2.5 * (last - k), line_sum, k))
+                    plan.append((21.8 + 8.6 * (last - k), line_sum, k))
                 elif k < u:
                     plan.append((21.7, line_x, k))
-                    plan.append((33.0, line_sum, k))
+                    plan.append((30.3, line_sum, k))
                 else:
                     plan.append((26.6, line_x, k))
+        if own == 0:
+            plan += [(4.4, a_side, 0), (6.2, a_side, 1)]
+        else:
+            plan += [(0.35, a_mate), (2.9, a_side, 2), (4.2, a_side, 3), (6.0, a_side, 0), (7.7, a_side, 1)]
         when = {}
-        for k in others:
-            hops = abs(k - u)
-            when[k] = 3.5 + 6.0 * (hops - 1)
-            plan.append((when[k], a_line, k, y, 0))
-            plan.append((when[k] + 1.7, a_line, k, y, 1))
-            plan.append((when[k] + 2.9, a_line, k, y, 2))
-            plan.append((when[k] + 4.2, a_line, k, there, 2))
-        queue = 4.7
-        for i in (0, 1):
+        for core_id in (0, 1):
+            moments = {}
             for k in others:
-                if u == 0 or abs(k - u) == 1:
-                    queue = max(queue, when[k] + 1.7 * i) + 1.75 if u else when[k] + 1.7 * i + 1.75
-                    when[k, i] = queue + (1.8 if u else 3.3)
-                    plan.append((when[k, i], a_over, k, i))
-        for i in (0, 1):
-            for k in others:
-                if u > 0 and abs(k - u) > 1:
-                    queue = max(queue, when[k] + 1.7 * i) + 1.75
-                    when[k, i] = queue + (1.8 if u else 3.3)
-                    plan.append((when[k, i], a_over, k, i))
+                hops = abs(k - u)
+                moments[k] = 4.35 * hops if core_id == 0 else 3.5 + 6.0 * (hops - 1)
+            queue, crossing = 4.7, 2.7 if core_id == 0 else 1.8
+            arrivals = sorted((moments[k] + 1.7 * i, k, i) for k in others for i in (0, 1))
+            for moment, k, i in arrivals:
+                queue = max(queue, moment) + 1.75
+                when[k, i] = max(when.get((k, i), 0), queue + crossing)
+                if core_id == own:
+                    plan.append((moment, a_line, k, y, i))
+                    plan.append((queue + crossing + 1.0, a_over, k, i))
+            if core_id == own == 1:
+                for k in others:
+                    for i in (2, 3):
+                        plan.append((moments[k] + 1.6 + 0.6 * i, a_line, k, y, i))
+                        plan.append((moments[k] + 2.8 + 0.6 * i, a_line, k, there, i))
         for i, k in enumerate([u] + others):
             done = 9.0 if i == 0 else when[k, 1] + 1.2 + 0.1 * i
             if i < depth - 1 or depth == 1:
@@ -547,7 +575,7 @@
         begin = done + 4.5
         if u == 0:
             plan.append((begin + 1.6, line_x, u))
-            for k, moment in zip(order[:-1], (done + 0.15, done + 0.3, begin + 1.55)):
+            for k, moment in zip(order[1:-1], (done + 0.15, done + 0.3)):
                 plan.append((moment, line_sum, k))
         plan.append((begin, b_part))
         for i, k in enumerate(b_order):
@@ -555,11 +583,11 @@
             plan.append((begin + 4.5 + 0.9 * i, b_side, k))
         begin = max(begin, 6.0 * last + 10.3)
         plan.append((begin + 9.5, b_line))
-        plan.append((begin + 13.9, line_sum, u))
-        plan.append((begin + 13.91, a_end))
-        plan.append((begin + 15.5, b_pass, u, there))
+        plan.append((begin + 12.9, line_sum, u))
+        plan.append((begin + 12.91, a_end))
+        plan.append((begin + 12.0, b_pass, u, there))
         for i, k in enumerate(others):
-            plan.append((begin + 12.0 + 0.9 * i, b_pass, k, y))
+            plan.append((begin + 12.1 + 0.01 * (last - i), b_pass, k, y))
             plan.append((begin + 14.0 + 0.9 * i, b_pass, k, there))
         plan.append((begin + 18.0, loss_end))
         plan.append((begin + 19.0, b_end))
@@ -571,9 +599,10 @@
             drain()
 
     for u in range((depth + 1) // 2):
-        @pl.when(jnp.minimum(z, last - z) == u)
-        def _():
-            run(u)
+        for own in (0, 1):
+            @pl.when((jnp.minimum(z, last - z) == u) & (c == own))
+            def _():
+                run(u, own)
 
 
 def finish_kernel(a_in, b_in, loss_in, a_out, b_out, loss_out, sems):
@@ -599,6 +628,7 @@
     scalars = pl.BlockSpec(memory_space=pltpu.SMEM)
     hbm = pl.BlockSpec(memory_space=pltpu.HBM)
     quarter, chunk = rank // 4, width // depth
+    quarter = rank * 3 // 8
     cut_g, cut_r = rows * 3 // 64 * 16, rows // 32 * 16
     grad_a, grad_b, loss = pl.pallas_call(
         functools.partial(fused_kernel, n, lengths.shape[0], lengths.shape[1], cut_g, cut_r),
@@ -621,17 +651,18 @@
             pltpu.VMEM((2 * depth, rows, rank), bf16),
             pltpu.VMEM((depth, cut_r, rank), bf16),
             pltpu.VMEM((2 * depth, cut_r, rank), bf16),
-            pltpu.VMEM((2, 2 * depth, rows - cut_r, rank), bf16),
+            pltpu.VMEM((2 * depth, 2, rows - cut_r, rank), bf16),
             pltpu.VMEM((rows - cut_r, rank), bf16),
             pltpu.VMEM((2, tokens, rank), f32),
-            pltpu.VMEM((tokens, rank), f32),
+            pltpu.VMEM((tokens, rank), bf16),
+            pltpu.VMEM((tokens, rank), bf16),
             pltpu.VMEM((tokens, rank), bf16),
             pltpu.VMEM((tokens, rank), bf16),
             pltpu.VMEM((tokens, rank), f32),
             pltpu.VMEM((tokens, rank), bf16),
             pltpu.VMEM((rank, width), f32),
             pltpu.VMEM((rank, width), bf16),
-            pltpu.VMEM((rank // 2, width), bf16),
+            pltpu.VMEM((rank * 3 // 4, width), bf16),
             pltpu.VMEM((quarter, width), bf16),
             pltpu.VMEM((quarter, width), bf16),
             pltpu.VMEM((quarter, width), bf16),
@@ -642,8 +673,8 @@
             pltpu.VMEM((8, 128), f32),
             pltpu.VMEM((depth, 8, 128), f32),
             pltpu.VMEM((1, 128), f32),
-            dma((7,)), dma((4,)), dma((6 * depth,)), dma((2 * depth,)),
-            dma((depth,)), dma((depth,)), dma((2 * depth,)), dma((2, 2 * depth)), dma((1,)),
+            dma((7,)), dma((4,)), dma((8 * depth,)), dma((2 * depth + 1,)),
+            dma((depth,)), dma((depth,)), dma((2 * depth,)), dma((2 * depth,)), dma((1,)),
             dma((2,)), dma((depth,)), dma((depth,)), dma((depth,)), dma((2 * depth + 1,)),
             dma((2,)), dma((depth,)),
         ],
@@ -692,6 +723,7 @@
         and activations.shape[0] % 128 == 0
         and ff % 128 == 0
         and 4 * rows % 128 == 0
+        and rows % 32 == 0
         and rows >= 64
         and width % (128 * (n // 4)) == 0
         and n % lengths.shape[0] == 0

time: 55.6 us -> 52.8 us (0.950)
  Pallas kernels: 54.8 us -> 51.2 us
    pallas_call x1, Pallas kernels: 53 us -> 49.5 us  [fused_local(): pl.pallas_call(functools.partial(fused_kernel, n, lengths.shape[0], lengt...]
where the time goes in v4:
time: 52.8 us; the launch traced here: 52.1 us
  Pallas kernels  51.2 us (97%)
  between operations  0.8 us (2%)
    pallas_call x1, Pallas kernels, fused_local(): pl.pallas_call(functools.partial(fused_kernel, n, lengths.shape[0], lengt...  49.5 us
    pallas_call x1, Pallas kernels, fused_local(): pl.pallas_call(finish_kernel, out_shape=(jax.ShapeDtypeStruct((rows, rank...  1.74 us

profile of v4, /device:TPU:1, one launch (start us, length us, event | category | flops | bytes accessed | tf_op | source)
XLA Modules:
  0.0 52.1 jit_solution(18189245744298417475)
XLA Ops:
  0.6 49.5 %fused.1 = (f32[864,128]{1,0:T(8,128)S(1)}, f32[128,2560]{1,0:T(8,128)S(1)}, f32[8,128]{1,0:T(8,128)S(1)}) custom-call(bf16[256,13824]{1,0:T(8,128)(2,1)} %act_hbm.1, bf16[256,2560]{1,0:T(8,128)(2,1)} %grad_hbm.1, bf16[864,128]{1,0:T(8,128)(2,1)} %bitcast.4, bf16[128,2560]{1,0:T(8,128)(2,1)} %b_hbm.1, f32[2,128]{1,0:T(2,128)} %bitcast.5, s32[1,16]{1,0:T(1,128)} %len_hbm.1, ...), custom_call_target="tpu_custom_call" | custom-call | tf_op jit(solution)/shard_map/fused/pallas_call | solution.py:633
  50.2 1.7 %finish.1 = (f32[864,128]{1,0:T(8,128)}, f32[128,2560]{1,0:T(8,128)}, f32[1,1]{1,0:T(1,128)}) custom-call(f32[864,128]{1,0:T(8,128)S(1)} %get-tuple-element.9.a_in, f32[128,2560]{1,0:T(8,128)S(1)} %get-tuple-element.10.b_in, f32[8,128]{1,0:T(8,128)S(1)} %get-tuple-element.11.loss_in), custom_call_target="tpu_custom_call" | custom-call | tf_op jit(solution)/shard_map/finish/pallas_call | solution.py:694

commit v5 on v4

--- a/solution.py
+++ b/solution.py
@@ -132,13 +132,15 @@
         pltpu.make_async_copy(s, d, loc.at[4 + i])
         for i, (s, d) in enumerate(((ratio_hbm, ratio_ref), (len_hbm, len_ref), (rew_hbm, rew_ref)))
     ]
+    load_a.start()
     barrier = pltpu.get_barrier_semaphore()
     for dev in [core, side] + [at((z + k) % depth, y, c) for k in range(1, depth)]:
         pl.semaphore_signal(barrier, inc=1, device_id=(dev, t), device_id_type=MESH)
     pl.semaphore_signal(barrier, inc=1, device_id=(p, 1 - t), device_id_type=MESH)
-    for copy in [load_a, load_g, load_b] + small + [load_x]:
+    for copy in [load_g, load_b] + small:
         copy.start()
     load_a.wait()
+    load_x.start()
     with jax.named_scope("barrier") if SCOPES else contextlib.nullcontext():
         pl.semaphore_wait(barrier, depth + 2)
     flip = (2 * z > last).astype(jnp.int32)
@@ -280,6 +282,9 @@
             low_s[...] = xs[1].astype(bf16)
             go(low_s, low_r, x_r.at[1], p, 1 - t)
 
+        def source_slot(k):
+            return z - (z > m(k)).astype(jnp.int32)
+
         def loss_one():
             go(ls.at[0], l1, l_r.at[0], core)
 
@@ -290,15 +295,15 @@
 
         def loss_three():
             got(l2, l_r.at[1])
-            lz[z] = ls[1] + l2[...]
+            ls[2] = ls[1] + l2[...]
             for k in others:
-                go(lz.at[z], lz.at[z], lz_r.at[z], z_dev(k))
+                go(ls.at[2], lz.at[source_slot(k)], lz_r.at[0], z_dev(k))
 
         def loss_end():
-            for k in others:
-                got(lz.at[m(k)], lz_r.at[m(k)])
-            total = lz[0]
-            for i in range(1, depth):
+            if last:
+                got(lz.at[pl.ds(0, last)], lz_r.at[0])
+            total = ls[2]
+            for i in range(last):
                 total = total + lz[i]
             out_loss[...] = fac[...] * total
 
@@ -387,15 +392,16 @@
             ref[...] = both(k, 1 - y, 0).astype(bf16)
             go(ref, rs2.at[m(k)], rs2_r.at[m(k)], side)
 
-        def line_slot(k, upward):
-            return (flip if upward else 1 - flip) * depth + m(k)
+        def line_slot(k, upward, final):
+            falling = (flip if upward else 1 - flip) if final else 0
+            return m(k) + falling * (depth - m(k))
 
         def sources(k):
             found = []
             if k >= u and down is not None:
-                found.append(line_slot(k, True))
+                found.append(line_slot(k, True, k == u))
             if k <= u and up is not None:
-                found.append(line_slot(k, False))
+                found.append(line_slot(k, False, k == u))
             return found
 
         def line_x(k):
@@ -408,7 +414,7 @@
                 ref = span(k, yy, c, 1)
                 if k != u:
                     ref[...] = total.astype(bf16)
-                    slot = line_slot(k, k > u)
+                    slot = line_slot(k, k > u, abs(k - u) == 1)
                     go(ref, rs3x.at[slot, b], rs3x_r.at[slot], z_dev(up if k > u else down))
                 elif b == 0:
                     ref[...] = total.astype(bf16)
@@ -427,7 +433,7 @@
             else:
                 ref = span(k, y, c, 0)
                 ref[...] = total.astype(bf16)
-                slot = line_slot(k, k > u)
+                slot = line_slot(k, k > u, abs(k - u) == 1)
                 go(ref, rs3.at[slot], rs3_r.at[slot], z_dev(up if k > u else down))
 
         def a_end():
@@ -483,7 +489,7 @@
                 gb[pl.ds(mine, quarter), cols] = total
             else:
                 gb3s[whole, cols] = total.astype(bf16)
-                go(gb3s.at[whole, cols], gb3.at[z, whole], g3_r.at[z], z_dev(k))
+                go(gb3s.at[whole, cols], gb3.at[source_slot(k), whole], g3_r.at[0], z_dev(k))
 
         def final(k, yy, cc):
             at_row = pl.multiple_of(bases[cc] + yy * quarters[cc], 16)
@@ -497,9 +503,10 @@
         def b_line():
             cols = cols_of(u)
             total = gb[pl.ds(mine, quarter), cols]
-            for k in others:
-                got(gb3.at[m(k), whole], g3_r.at[m(k)])
-                total = total + gb3[m(k), whole, :].astype(f32)
+            if last:
+                got(gb3.at[pl.ds(0, last), whole], g3_r.at[0])
+            for i in range(last):
+                total = total + gb3[i, whole, :].astype(f32)
             scaled = jnp.full((1, 128), adapter_scale_factor) * fac[...]
             fin[pl.ds(mine, quarter), cols] = (scaled[:, :1] * total).astype(bf16)
             b_send(u, y, *[z_dev(k) for k in others[::-1]], side, core)
@@ -605,14 +612,14 @@
                 run(u, own)
 
 
-def finish_kernel(a_in, b_in, loss_in, a_out, b_out, loss_out, sems):
+def finish_kernel(a_in, b_in, loss_in, a_out, b_out, loss_out, loss_s, sems):
+    loss_s[0, 0] = loss_in[0, 0]
     copies = [
         pltpu.make_async_copy(s, d, sems.at[i])
-        for i, (s, d) in enumerate(((a_in, a_out), (b_in, b_out)))
+        for i, (s, d) in enumerate(((b_in, b_out), (a_in, a_out), (loss_s, loss_out)))
     ]
     for copy in copies:
         copy.start()
-    loss_out[0, 0] = loss_in[0, 0]
     for copy in copies:
         copy.wait()
 
@@ -650,8 +657,8 @@
             pltpu.VMEM((ff, rank), bf16),
             pltpu.VMEM((2 * depth, rows, rank), bf16),
             pltpu.VMEM((depth, cut_r, rank), bf16),
-            pltpu.VMEM((2 * depth, cut_r, rank), bf16),
-            pltpu.VMEM((2 * depth, 2, rows - cut_r, rank), bf16),
+            pltpu.VMEM((depth + 1, cut_r, rank), bf16),
+            pltpu.VMEM((depth + 1, 2, rows - cut_r, rank), bf16),
             pltpu.VMEM((rows - cut_r, rank), bf16),
             pltpu.VMEM((2, tokens, rank), f32),
             pltpu.VMEM((tokens, rank), bf16),
@@ -668,15 +675,15 @@
             pltpu.VMEM((quarter, width), bf16),
             pltpu.VMEM((depth, quarter, chunk), bf16),
             pltpu.VMEM((rank, width), bf16),
-            pltpu.VMEM((2, 8, 128), f32),
+            pltpu.VMEM((3, 8, 128), f32),
             pltpu.VMEM((8, 128), f32),
             pltpu.VMEM((8, 128), f32),
             pltpu.VMEM((depth, 8, 128), f32),
             pltpu.VMEM((1, 128), f32),
             dma((7,)), dma((4,)), dma((8 * depth,)), dma((2 * depth + 1,)),
-            dma((depth,)), dma((depth,)), dma((2 * depth,)), dma((2 * depth,)), dma((1,)),
-            dma((2,)), dma((depth,)), dma((depth,)), dma((depth,)), dma((2 * depth + 1,)),
-            dma((2,)), dma((depth,)),
+            dma((depth,)), dma((depth,)), dma((depth + 1,)), dma((depth + 1,)), dma((1,)),
+            dma((2,)), dma((depth,)), dma((depth,)), dma((1,)), dma((2 * depth + 1,)),
+            dma((2,)), dma((1,)),
         ],
         compiler_params=pltpu.CompilerParams(
             collective_id=0, has_side_effects=True, vmem_limit_bytes=48 * 1024 * 1024
@@ -699,8 +706,8 @@
             jax.ShapeDtypeStruct((1, 1), f32),
         ),
         in_specs=[vmem, vmem, vmem],
-        out_specs=(hbm, hbm, scalars),
-        scratch_shapes=[dma((2,))],
+        out_specs=(hbm, hbm, hbm),
+        scratch_shapes=[pltpu.SMEM((1, 1), f32), dma((3,))],
         compiler_params=pltpu.CompilerParams(vmem_limit_bytes=4 * 1024 * 1024),
         name="finish",
     )(grad_a, grad_b, loss)

time: 52.8 us -> 52.3 us (level)
  no operation moved by 1% of the time
where the time goes in v5:
time: 52.3 us; the launch traced here: 51.5 us
  Pallas kernels  50.7 us (97%)
  between operations  0.8 us (2%)
    pallas_call x1, Pallas kernels, fused_local(): pl.pallas_call(functools.partial(fused_kernel, n, lengths.shape[0], lengt...  49.4 us
    pallas_call x1, Pallas kernels, fused_local(): pl.pallas_call(finish_kernel, out_shape=(jax.ShapeDtypeStruct((rows, rank...  1.23 us

profile of v5, /device:TPU:1, one launch (start us, length us, event | category | flops | bytes accessed | tf_op | source)
XLA Modules:
  0.0 51.5 jit_solution(14859203455027811471)
XLA Ops:
  0.6 49.4 %fused.1 = (f32[864,128]{1,0:T(8,128)S(1)}, f32[128,2560]{1,0:T(8,128)S(1)}, f32[8,128]{1,0:T(8,128)S(1)}) custom-call(bf16[256,13824]{1,0:T(8,128)(2,1)} %act_hbm.1, bf16[256,2560]{1,0:T(8,128)(2,1)} %grad_hbm.1, bf16[864,128]{1,0:T(8,128)(2,1)} %bitcast.4, bf16[128,2560]{1,0:T(8,128)(2,1)} %b_hbm.1, f32[2,128]{1,0:T(2,128)} %bitcast.5, s32[1,16]{1,0:T(1,128)} %len_hbm.1, ...), custom_call_target="tpu_custom_call" | custom-call | tf_op jit(solution)/shard_map/fused/pallas_call | solution.py:640
  50.1 1.2 %finish.1 = (f32[864,128]{1,0:T(8,128)}, f32[128,2560]{1,0:T(8,128)}, f32[1,1]{1,0:T(1,128)}) custom-call(f32[864,128]{1,0:T(8,128)S(1)} %get-tuple-element.9.a_in, f32[128,2560]{1,0:T(8,128)S(1)} %get-tuple-element.10.b_in, f32[8,128]{1,0:T(8,128)S(1)} %get-tuple-element.11.loss_in), custom_call_target="tpu_custom_call" | custom-call | tf_op jit(solution)/shard_map/finish/pallas_call | solution.py:701
